TPU v7x, 768 devices: a whole 4x8x12 slice. The times are simulated.
768 devices in a mesh: dp: 48 (over y_lo, z), section: 8 (over x, core), tensor: 2 (over y_hi).
Axes of the slice: x: 4, y: 8 (y_hi: 2, y_lo: 4; y = y_hi * 4 + y_lo), z: 12, core: 2. Of those that a mesh axis runs over, the one named last changes fastest.
Arguments:
- hidden: bfloat16 [18432, 8192], P(('dp', 'section', 'tensor')), may hold values from -6 to 6
- proj_weight: bfloat16 [8192, 8192], P(None, ('section', 'tensor')), may hold values from -0.0625 to 0.0625
- proj_bias: bfloat16 [8192], P(('section', 'tensor')), may hold values from -3 to 3
- route: int32 [18432, 1], P(('dp', 'section', 'tensor')), may hold values from 0 to 47; in each aligned block of 24 rows (0 to 23, 24 to 47, ...) at most 2 rows name the same one
- text: bfloat16 [73728, 8192], P(('dp', 'section', 'tensor')), may hold values from -6 to 6
- norm_gain: bfloat16 [8192], replicated, may hold values from 0.5 to 1.5
Outputs:
- normed: bfloat16 [73728, 8192], P(('dp', 'section', 'tensor'))
Inputs may be any that keep to these rules, and one draw needn't show every extreme that they name: `route`: among the rows of one device no replica is named more than 2 times; some device reaches 2.
All inputs are finite; a program needn't handle non-finite values.
Results may differ from a plain program's by a relative error of at most 0.0031.
Values may be sent and summed in bfloat16 or wider, within the bound.
No kernel may reach another device: no remote copies, remote signals or barrier semaphores. Data moves between devices by JAX's collectives and lax.ppermute only.
A program may use at most 64 MiB of HBM per device.

v0:
```python
import functools

import jax
import jax.numpy as jnp
from jax import lax
from jax.experimental import pallas as pl
from jax.experimental.pallas import tpu as pltpu
from jax.sharding import PartitionSpec as P


EMPTY = 2.0**100
NX = 4
GRANT = 16 * 1024 * 1024


def shift_x(block, by):
    n = lax.axis_size("section") // 2
    pairs = [(2 * x + c, 2 * ((x + by) % n) + c) for x in range(n) for c in range(2)]
    return lax.ppermute(block, "section", pairs)


def swap_core(block):
    n = lax.axis_size("section")
    return lax.ppermute(block, "section", [(i, i ^ 1) for i in range(n)])


def project_kernel(partner, swapped, lhs_ref, w_ref, bias_ref, *rest):
    out_ref, acc = rest[-2:]
    depth = lhs_ref.shape[1]
    step = 1024
    acc[...] = jnp.zeros_like(acc)

    @pl.loop(0, depth // step)
    def _(k):
        at = pl.ds(pl.multiple_of(k * step, step), step)
        acc[...] += jnp.dot(lhs_ref[:, at], w_ref[at, :], preferred_element_type=jnp.float32)

    if len(rest) == 3:
        out_ref[...] = rest[0][...]
    section = lax.axis_index("section")
    tensor = lax.axis_index("tensor")
    x, core = section // 2, section % 2
    t = (1 - tensor) if partner else tensor
    c = (1 - core) if swapped else core
    rows = out_ref.shape[1]
    bias = bias_ref[...].astype(jnp.float32)
    for k in range(NX):
        dst = (lax.rem(x - k + NX, NX) * 2 + c) * 2 + t
        out_ref[dst] = (acc[k * rows : (k + 1) * rows, :] + bias).astype(out_ref.dtype)


def project(lhs, weight, bias, partner, swapped, base=None):
    rows, depth = lhs.shape
    width = weight.shape[1]
    operands = [lhs, weight, bias] + ([] if base is None else [base])
    return pl.pallas_call(
        functools.partial(project_kernel, partner, swapped),
        in_specs=[pl.BlockSpec(memory_space=pltpu.VMEM)] * len(operands),
        out_specs=pl.BlockSpec(memory_space=pltpu.VMEM),
        out_shape=jax.ShapeDtypeStruct((4 * NX, rows // NX, width), jnp.bfloat16),
        scratch_shapes=[pltpu.VMEM((rows, width), jnp.float32)],
        compiler_params=pltpu.CompilerParams(vmem_limit_bytes=GRANT),
        cost_estimate=pl.CostEstimate(
            flops=2 * rows * depth * width,
            bytes_accessed=2 * (rows * depth + depth * width + rows * width),
            transcendentals=0,
        ),
        name="project",
    )(*operands)


def pack_kernel(route_ref, tokens_ref, out_ref):
    blocks, rows, width = tokens_ref.shape
    slots = out_ref.shape[0]
    first = lax.broadcasted_iota(jnp.int32, (rows, rows), 0)
    second = lax.broadcasted_iota(jnp.int32, (rows, rows), 1)
    down = route_ref[...].astype(jnp.float32)
    across = jnp.sum(jnp.where(first == second, down, 0.0), axis=0, keepdims=True)
    earlier = jnp.where((first < second) & (down == across), 1.0, 0.0)
    slot = 2.0 * across + jnp.sum(earlier, axis=0, keepdims=True)
    ids = lax.broadcasted_iota(jnp.int32, (slots, rows), 0).astype(jnp.float32)
    pick = jnp.where(ids == slot, 1.0, 0.0)
    mark = jnp.where(jnp.sum(pick, axis=1, keepdims=True) > 0.0, 0.0, EMPTY)
    pick = pick.astype(jnp.bfloat16)
    for k in range(blocks):
        moved = jnp.dot(pick, tokens_ref[k], preferred_element_type=jnp.float32)
        out_ref[:, k * width : (k + 1) * width] = (moved + mark).astype(out_ref.dtype)


def pack(route, tokens, slots):
    blocks, rows, width = tokens.shape
    return pl.pallas_call(
        pack_kernel,
        in_specs=[pl.BlockSpec(memory_space=pltpu.VMEM)] * 2,
        out_specs=pl.BlockSpec(memory_space=pltpu.VMEM),
        out_shape=jax.ShapeDtypeStruct((slots, blocks * width), jnp.bfloat16),
        cost_estimate=pl.CostEstimate(
            flops=2 * slots * rows * blocks * width,
            bytes_accessed=2 * (slots + rows) * blocks * width,
            transcendentals=0,
        ),
        compiler_params=pltpu.CompilerParams(vmem_limit_bytes=GRANT),
        name="pack",
    )(route, tokens)


def finish_kernel(inbox_ref, text_ref, gain_ref, out_ref, merged):
    slots, width = inbox_ref.shape
    rows = text_ref.shape[0]
    first = lax.broadcasted_iota(jnp.int32, (slots, slots), 0)
    second = lax.broadcasted_iota(jnp.int32, (slots, slots), 1)
    down = jnp.where(inbox_ref[:, 0:128].astype(jnp.float32)[:, 0:1] < EMPTY / 2, 1.0, 0.0)
    across = jnp.sum(jnp.where(first == second, down, 0.0), axis=0, keepdims=True)
    place = jnp.sum(jnp.where(first < second, down, 0.0), axis=0, keepdims=True)
    ids = lax.broadcasted_iota(jnp.int32, (rows, slots), 0).astype(jnp.float32)
    pick = jnp.where((ids == place) & (across > 0.0), 1.0, 0.0)
    is_image = jnp.sum(pick, axis=1, keepdims=True) > 0.0
    pick = pick.astype(jnp.bfloat16)
    step = 1024
    square = jnp.zeros((rows, 1), jnp.float32)
    for k in range(width // step):
        at = slice(k * step, (k + 1) * step)
        moved = jnp.dot(pick, inbox_ref[:, at], preferred_element_type=jnp.float32)
        values = jnp.where(is_image, moved, text_ref[:, at].astype(jnp.float32))
        merged[:, at] = values
        square += jnp.sum(values * values, axis=1, keepdims=True)
    scale_inv = lax.rsqrt(square * (1.0 / width) + 1e-05)
    for k in range(width // step):
        at = slice(k * step, (k + 1) * step)
        gain = gain_ref[:, at].astype(jnp.float32)
        out_ref[:, at] = (merged[:, at] * scale_inv * gain).astype(out_ref.dtype)


def finish(inbox, text, gain):
    rows, width = text.shape
    return pl.pallas_call(
        finish_kernel,
        in_specs=[pl.BlockSpec(memory_space=pltpu.VMEM)] * 3,
        out_specs=pl.BlockSpec(memory_space=pltpu.VMEM),
        out_shape=jax.ShapeDtypeStruct((rows, width), jnp.bfloat16),
        scratch_shapes=[pltpu.VMEM((rows, width), jnp.float32)],
        cost_estimate=pl.CostEstimate(
            flops=2 * rows * inbox.shape[0] * width,
            bytes_accessed=2 * (2 * rows + inbox.shape[0]) * width,
            transcendentals=rows,
        ),
        compiler_params=pltpu.CompilerParams(vmem_limit_bytes=GRANT),
        name="finish",
    )(inbox, text, gain)


def per_device(hidden, proj_weight, proj_bias, route, text, norm_gain):
    replicas = lax.axis_size("dp")
    _, width = hidden.shape
    capacity = 2
    bias = proj_bias[None, :]
    partner = lax.ppermute(hidden, "tensor", [(0, 1), (1, 0)])

    def along_x(block):
        pieces = [block]
        for by in (1, 2, -1):
            pieces.append(shift_x(block, by))
        return jnp.concatenate(pieces, axis=0)

    blocks = None
    for name, block in (("own", hidden), ("other", partner)):
        mine = along_x(block)
        blocks = project(mine, proj_weight, bias, name == "other", False, blocks)
        theirs = swap_core(mine)
        blocks = project(theirs, proj_weight, bias, name == "other", True, blocks)
    own = lax.all_to_all(blocks, ("section", "tensor"), split_axis=0, concat_axis=0, tiled=True)
    outbox = pack(route, own, replicas * capacity)
    inbox = lax.all_to_all(
        outbox.reshape(replicas, capacity, width), "dp", split_axis=0, concat_axis=0, tiled=True
    )
    return finish(inbox.reshape(replicas * capacity, width), text, norm_gain[None, :])


def solution(mesh):
    in_specs = (
        P(("dp", "section", "tensor"), None),
        P(None, ("section", "tensor")),
        P(("section", "tensor")),
        P(("dp", "section", "tensor"), None),
        P(("dp", "section", "tensor"), None),
        P(),
    )
    out_specs = P(("dp", "section", "tensor"), None)
    return jax.shard_map(
        per_device, mesh=mesh, in_specs=in_specs, out_specs=out_specs, check_vma=False
    )
```

profile of v0, /device:TPU:8, one launch (start us, length us, event | category | flops | bytes accessed | tf_op | source)
XLA Modules:
  0.0 182.4 jit_solution(14463695490751104626)
XLA Ops:
  0.0 6.8 %collective-permute-start = (bf16[24,8192]{1,0:T(8,128)(2,1)}, bf16[24,8192]{1,0:T(8,128)(2,1)S(1)}, u32[]{:S(2)}, u32[]{:S(2)}) collective-permute-start(bf16[24,8192]{1,0:T(8,128)(2,1)} %param.6), channel_id=1, source_target_pairs={{0,1},{1,0},{2,3},{3,2},{4,5},{5,4},{6,7},{7,6},{8,9},{9,8},{10,11... | collective-permute-start | bytes 1179656 | tf_op jit(solution)/shard_map/ppermute | solution.py:157
  6.8 3.4 %collective-permute-start.5 = (bf16[24,8192]{1,0:T(8,128)(2,1)}, bf16[24,8192]{1,0:T(8,128)(2,1)S(1)}, u32[]{:S(2)}, u32[]{:S(2)}) collective-permute-start(bf16[24,8192]{1,0:T(8,128)(2,1)} %param.6), channel_id=1, source_target_pairs={{0,4},{2,6},{4,8},{6,10},{8,12},{10,14},{12,0},{14,2},{1,5},{3,7},... | collective-permute-start | bytes 1179656 | tf_op jit(solution)/shard_map/ppermute | solution.py:19
  10.2 4.6 %collective-permute-start.6 = (bf16[24,8192]{1,0:T(8,128)(2,1)}, bf16[24,8192]{1,0:T(8,128)(2,1)S(1)}, u32[]{:S(2)}, u32[]{:S(2)}) collective-permute-start(bf16[24,8192]{1,0:T(8,128)(2,1)} %param.6), channel_id=1, source_target_pairs={{0,8},{2,10},{4,12},{6,14},{8,0},{10,2},{12,4},{14,6},{1,9},{3,11}... | collective-permute-start | bytes 1179656 | tf_op jit(solution)/shard_map/ppermute | solution.py:19
  14.9 3.3 %collective-permute-start.7 = (bf16[24,8192]{1,0:T(8,128)(2,1)}, bf16[24,8192]{1,0:T(8,128)(2,1)S(1)}, u32[]{:S(2)}, u32[]{:S(2)}) collective-permute-start(bf16[24,8192]{1,0:T(8,128)(2,1)} %param.6), channel_id=1, source_target_pairs={{0,12},{2,14},{4,0},{6,2},{8,4},{10,6},{12,8},{14,10},{1,13},{3,15... | collective-permute-start | bytes 1179656 | tf_op jit(solution)/shard_map/ppermute | solution.py:19
  18.2 1.0 constant_dynamic-update-slice_fusion.7
  19.3 1.9 %collective-permute-done.5 = bf16[24,8192]{1,0:T(8,128)(2,1)S(1)} collective-permute-done((bf16[24,8192]{1,0:T(8,128)(2,1)}, bf16[24,8192]{1,0:T(8,128)(2,1)S(1)}, u32[]{:S(2)}, u32[]{:S(2)}) %collective-permute-start.5) | collective-permute-done | bytes 393248 | tf_op jit(solution)/shard_map/ppermute | solution.py:19
  21.2 9.0 %collective-permute-done.6 = bf16[24,8192]{1,0:T(8,128)(2,1)S(1)} collective-permute-done((bf16[24,8192]{1,0:T(8,128)(2,1)}, bf16[24,8192]{1,0:T(8,128)(2,1)S(1)}, u32[]{:S(2)}, u32[]{:S(2)}) %collective-permute-start.6) | collective-permute-done | bytes 393248 | tf_op jit(solution)/shard_map/ppermute | solution.py:19
  30.2 1.5 collective-permute-done.7
  31.7 0.0 copy-start.4
  31.7 1.9 %collective-permute-start.8 = (bf16[96,8192]{1,0:T(8,128)(2,1)S(1)}, bf16[96,8192]{1,0:T(8,128)(2,1)S(1)}, u32[]{:S(2)}, u32[]{:S(2)}) collective-permute-start(bf16[96,8192]{1,0:T(8,128)(2,1)S(1)} %constant_dynamic-update-slice_fusion.4.lhs_ref), channel_id=1, source_target_pairs={{0,2},{2,0},{4,6},{6,4},{8,10},{10,8},{12,14},{14,12},{1,3},{3,1},... | collective-permute-start | bytes 4718600 | tf_op jit(solution)/shard_map/ppermute | solution.py:24
  33.7 0.0 collective-permute-done
  33.7 4.3 %collective-permute-start.1 = (bf16[24,8192]{1,0:T(8,128)(2,1)S(1)}, bf16[24,8192]{1,0:T(8,128)(2,1)S(1)}, u32[]{:S(2)}, u32[]{:S(2)}) collective-permute-start(bf16[24,8192]{1,0:T(8,128)(2,1)S(1)} %collective-permute-done), channel_id=1, source_target_pairs={{0,4},{2,6},{4,8},{6,10},{8,12},{10,14},{12,0},{14,2},{1,5},{3,7},... | collective-permute-start | bytes 1179656 | tf_op jit(solution)/shard_map/ppermute | solution.py:19
  38.0 3.6 %collective-permute-start.2 = (bf16[24,8192]{1,0:T(8,128)(2,1)S(1)}, bf16[24,8192]{1,0:T(8,128)(2,1)S(1)}, u32[]{:S(2)}, u32[]{:S(2)}) collective-permute-start(bf16[24,8192]{1,0:T(8,128)(2,1)S(1)} %collective-permute-done), channel_id=1, source_target_pairs={{0,8},{2,10},{4,12},{6,14},{8,0},{10,2},{12,4},{14,6},{1,9},{3,11}... | collective-permute-start | bytes 1179656 | tf_op jit(solution)/shard_map/ppermute | solution.py:19
  41.6 3.5 %collective-permute-start.3 = (bf16[24,8192]{1,0:T(8,128)(2,1)S(1)}, bf16[24,8192]{1,0:T(8,128)(2,1)S(1)}, u32[]{:S(2)}, u32[]{:S(2)}) collective-permute-start(bf16[24,8192]{1,0:T(8,128)(2,1)S(1)} %collective-permute-done), channel_id=1, source_target_pairs={{0,12},{2,14},{4,0},{6,2},{8,4},{10,6},{12,8},{14,10},{1,13},{3,15... | collective-permute-start | bytes 1179656 | tf_op jit(solution)/shard_map/ppermute | solution.py:19
  45.1 3.2 %collective-permute-done.1 = bf16[24,8192]{1,0:T(8,128)(2,1)S(1)} collective-permute-done((bf16[24,8192]{1,0:T(8,128)(2,1)S(1)}, bf16[24,8192]{1,0:T(8,128)(2,1)S(1)}, u32[]{:S(2)}, u32[]{:S(2)}) %collective-permute-start.1) | collective-permute-done | bytes 393248 | tf_op jit(solution)/shard_map/ppermute | solution.py:19
  48.3 9.3 %collective-permute-done.2 = bf16[24,8192]{1,0:T(8,128)(2,1)S(1)} collective-permute-done((bf16[24,8192]{1,0:T(8,128)(2,1)S(1)}, bf16[24,8192]{1,0:T(8,128)(2,1)S(1)}, u32[]{:S(2)}, u32[]{:S(2)}) %collective-permute-start.2) | collective-permute-done | bytes 393248 | tf_op jit(solution)/shard_map/ppermute | solution.py:19
  57.6 1.7 collective-permute-done.3
  59.3 1.9 %collective-permute-start.4 = (bf16[96,8192]{1,0:T(8,128)(2,1)S(1)}, bf16[96,8192]{1,0:T(8,128)(2,1)S(1)}, u32[]{:S(2)}, u32[]{:S(2)}) collective-permute-start(bf16[96,8192]{1,0:T(8,128)(2,1)S(1)} %constant_dynamic-update-slice_fusion.lhs_ref), channel_id=1, source_target_pairs={{0,2},{2,0},{4,6},{6,4},{8,10},{10,8},{12,14},{14,12},{1,3},{3,1},... | collective-permute-start | bytes 4718600 | tf_op jit(solution)/shard_map/ppermute | solution.py:24
  61.2 0.0 copy-done.4
  61.3 0.0 copy-start
  61.3 3.4 %copy-done = bf16[8192,512]{1,0:T(8,128)(2,1)S(1)} copy-done((bf16[8192,512]{1,0:T(8,128)(2,1)S(1)}, bf16[8192,512]{1,0:T(8,128)(2,1)}, u32[]{:S(2)}) %copy-start) | copy-done | bytes 8388632
  64.6 0.0 copy-start.1
  64.7 2.5 %project.4.rest_0_ = bf16[16,24,512]{2,1,0:T(8,128)(2,1)S(1)} custom-call(bf16[96,8192]{1,0:T(8,128)(2,1)S(1)} %constant_dynamic-update-slice_fusion.4.lhs_ref, bf16[8192,512]{1,0:T(8,128)(2,1)S(1)} %copy-done, bf16[1,512]{1,0:T(2,128)(2,1)S(1)} %broadcast_in_dim.6.bias_ref), custom_call_target="tpu_custom_call" | custom-call | flops 805306368 | bytes 10059776 | tf_op jit(solution)/shard_map/project/pallas_call | solution.py:56
  67.2 0.0 collective-permute-done.8.lhs_ref
  67.2 0.8 copy-done.1
  68.0 2.5 %project.5.rest_0_ = bf16[16,24,512]{2,1,0:T(8,128)(2,1)S(1)} custom-call(bf16[96,8192]{1,0:T(8,128)(2,1)S(1)} %collective-permute-done.8.lhs_ref, bf16[8192,512]{1,0:T(8,128)(2,1)S(1)} %copy-done.1, bf16[1,512]{1,0:T(2,128)(2,1)S(1)} %broadcast_in_dim.6.bias_ref, bf16[16,24,512]{2,1,0:T(8,128)(2,1)S(1)} %project.4.rest_0_), custom_call_target="tpu_custom_call" | custom-call | flops 805306368 | bytes 10059776 | tf_op jit(solution)/shard_map/project/pallas_call | solution.py:56
  70.5 2.5 %project.6.rest_0_ = bf16[16,24,512]{2,1,0:T(8,128)(2,1)S(1)} custom-call(bf16[96,8192]{1,0:T(8,128)(2,1)S(1)} %constant_dynamic-update-slice_fusion.lhs_ref, bf16[8192,512]{1,0:T(8,128)(2,1)S(1)} %copy-done.1, bf16[1,512]{1,0:T(2,128)(2,1)S(1)} %broadcast_in_dim.6.bias_ref, bf16[16,24,512]{2,1,0:T(8,128)(2,1)S(1)} %project.5.rest_0_), custom_call_target="tpu_custom_call" | custom-call | flops 805306368 | bytes 10059776 | tf_op jit(solution)/shard_map/project/pallas_call | solution.py:56
  73.0 0.0 copy-start.5
  73.0 0.0 collective-permute-done.4.lhs_ref
  73.0 3.2 %project.7 = bf16[16,24,512]{2,1,0:T(8,128)(2,1)} custom-call(bf16[96,8192]{1,0:T(8,128)(2,1)S(1)} %collective-permute-done.4.lhs_ref, bf16[8192,512]{1,0:T(8,128)(2,1)S(1)} %copy-done.1, bf16[1,512]{1,0:T(2,128)(2,1)S(1)} %broadcast_in_dim.6.bias_ref, bf16[16,24,512]{2,1,0:T(8,128)(2,1)S(1)} %project.6.rest_0_), custom_call_target="tpu_custom_call" | custom-call | flops 805306368 | bytes 10059776 | tf_op jit(solution)/shard_map/project/pallas_call | solution.py:56
  76.2 4.9 %all-to-all-start = ((bf16[16,24,512]{2,1,0:T(8,128)(2,1)}), bf16[16,24,512]{2,1,0:T(8,128)(2,1)S(1)}, u32[]{:S(2)}, u32[]{:S(2)}) async-start(bf16[16,24,512]{2,1,0:T(8,128)(2,1)} %project.7), calls=%async_computation | async-start | bytes 786432 | tf_op jit(solution)/shard_map/all_to_all | solution.py:171
  81.2 0.0 copy-done.5
  81.2 0.1 copy.7.route_ref
  81.3 15.0 %all-to-all-done.tokens_ref = bf16[16,24,512]{2,1,0:T(8,128)(2,1)S(1)} async-done(((bf16[16,24,512]{2,1,0:T(8,128)(2,1)}), bf16[16,24,512]{2,1,0:T(8,128)(2,1)S(1)}, u32[]{:S(2)}, u32[]{:S(2)}) %all-to-all-start) | async-done | bytes 393248 | tf_op jit(solution)/shard_map/all_to_all | solution.py:171
  96.3 0.6 pack.1
  96.9 2.3 %reshape.6 = bf16[48,2,8192]{2,1,0:T(2,128)(2,1)} reshape(bf16[96,8192]{1,0:T(8,128)(2,1)S(1)} %pack.1) | data formatting | bytes 3145728 | tf_op jit(solution)/shard_map/reshape | solution.py:174
  99.2 0.0 copy-start.3
  99.2 19.2 %all-to-all-start.1 = ((bf16[48,2,8192]{2,1,0:T(2,128)(2,1)}), bf16[48,2,8192]{2,1,0:T(2,128)(2,1)}, u32[]{:S(2)}, u32[]{:S(2)}) async-start(bf16[48,2,8192]{2,1,0:T(2,128)(2,1)} %reshape.6), calls=%async_computation.1 | async-start | bytes 3145728 | tf_op jit(solution)/shard_map/all_to_all | solution.py:173
  118.4 0.0 copy-done.3
  118.4 0.0 copy-start.2
  118.4 58.9 %all-to-all-done.1 = bf16[48,2,8192]{2,1,0:T(2,128)(2,1)} async-done(((bf16[48,2,8192]{2,1,0:T(2,128)(2,1)}), bf16[48,2,8192]{2,1,0:T(2,128)(2,1)}, u32[]{:S(2)}, u32[]{:S(2)}) %all-to-all-start.1) | async-done | bytes 1572896 | tf_op jit(solution)/shard_map/all_to_all | solution.py:173
  177.4 2.5 %reshape.7.inbox_ref = bf16[96,8192]{1,0:T(8,128)(2,1)S(1)} reshape(bf16[48,2,8192]{2,1,0:T(2,128)(2,1)} %all-to-all-done.1) | data formatting | bytes 3145728 | tf_op jit(solution)/shard_map/reshape | solution.py:176
  179.9 0.0 copy-done.2
  179.9 2.5 %finish.1 = bf16[96,8192]{1,0:T(8,128)(2,1)} custom-call(bf16[96,8192]{1,0:T(8,128)(2,1)S(1)} %reshape.7.inbox_ref, bf16[96,8192]{1,0:T(8,128)(2,1)S(1)} %copy-done.2, bf16[1,8192]{1,0:T(2,128)(2,1)S(1)} %broadcast_in_dim.7.gain_ref), custom_call_target="tpu_custom_call" | custom-call | flops 150994944 | bytes 4718592 | tf_op jit(solution)/shard_map/finish/pallas_call | solution.py:136
  (9 shorter events, 0.2 us)
Async XLA Ops:
  0.0 33.7 %collective-permute-start = (bf16[24,8192]{1,0:T(8,128)(2,1)}, bf16[24,8192]{1,0:T(8,128)(2,1)S(1)}, u32[]{:S(2)}, u32[]{:S(2)}) collective-permute-start(bf16[24,8192]{1,0:T(8,128)(2,1)} %param.6), channel_id=1, source_target_pairs={{0,1},{1,0},{2,3},{3,2},{4,5},{5,4},{6,7},{7,6},{8,9},{9,8},{10,11... | collective-permute-start | bytes 1179656 | tf_op jit(solution)/shard_map/ppermute | solution.py:157
  6.8 14.3 %collective-permute-start.5 = (bf16[24,8192]{1,0:T(8,128)(2,1)}, bf16[24,8192]{1,0:T(8,128)(2,1)S(1)}, u32[]{:S(2)}, u32[]{:S(2)}) collective-permute-start(bf16[24,8192]{1,0:T(8,128)(2,1)} %param.6), channel_id=1, source_target_pairs={{0,4},{2,6},{4,8},{6,10},{8,12},{10,14},{12,0},{14,2},{1,5},{3,7},... | collective-permute-start | bytes 1179656 | tf_op jit(solution)/shard_map/ppermute | solution.py:19
  10.2 19.9 %collective-permute-start.6 = (bf16[24,8192]{1,0:T(8,128)(2,1)}, bf16[24,8192]{1,0:T(8,128)(2,1)S(1)}, u32[]{:S(2)}, u32[]{:S(2)}) collective-permute-start(bf16[24,8192]{1,0:T(8,128)(2,1)} %param.6), channel_id=1, source_target_pairs={{0,8},{2,10},{4,12},{6,14},{8,0},{10,2},{12,4},{14,6},{1,9},{3,11}... | collective-permute-start | bytes 1179656 | tf_op jit(solution)/shard_map/ppermute | solution.py:19
  14.9 16.8 %collective-permute-start.7 = (bf16[24,8192]{1,0:T(8,128)(2,1)}, bf16[24,8192]{1,0:T(8,128)(2,1)S(1)}, u32[]{:S(2)}, u32[]{:S(2)}) collective-permute-start(bf16[24,8192]{1,0:T(8,128)(2,1)} %param.6), channel_id=1, source_target_pairs={{0,12},{2,14},{4,0},{6,2},{8,4},{10,6},{12,8},{14,10},{1,13},{3,15... | collective-permute-start | bytes 1179656 | tf_op jit(solution)/shard_map/ppermute | solution.py:19
  31.7 29.5 %copy-start.4 = (bf16[512]{0:T(512)(128)(2,1)S(1)}, bf16[512]{0:T(512)(128)(2,1)}, u32[]{:S(2)}) copy-start(bf16[512]{0:T(512)(128)(2,1)} %param.8) | copy-start | bytes 3076
  31.7 35.5 %collective-permute-start.8 = (bf16[96,8192]{1,0:T(8,128)(2,1)S(1)}, bf16[96,8192]{1,0:T(8,128)(2,1)S(1)}, u32[]{:S(2)}, u32[]{:S(2)}) collective-permute-start(bf16[96,8192]{1,0:T(8,128)(2,1)S(1)} %constant_dynamic-update-slice_fusion.4.lhs_ref), channel_id=1, source_target_pairs={{0,2},{2,0},{4,6},{6,4},{8,10},{10,8},{12,14},{14,12},{1,3},{3,1},... | collective-permute-start | bytes 4718600 | tf_op jit(solution)/shard_map/ppermute | solution.py:24
  33.7 14.6 %collective-permute-start.1 = (bf16[24,8192]{1,0:T(8,128)(2,1)S(1)}, bf16[24,8192]{1,0:T(8,128)(2,1)S(1)}, u32[]{:S(2)}, u32[]{:S(2)}) collective-permute-start(bf16[24,8192]{1,0:T(8,128)(2,1)S(1)} %collective-permute-done), channel_id=1, source_target_pairs={{0,4},{2,6},{4,8},{6,10},{8,12},{10,14},{12,0},{14,2},{1,5},{3,7},... | collective-permute-start | bytes 1179656 | tf_op jit(solution)/shard_map/ppermute | solution.py:19
  38.0 19.6 %collective-permute-start.2 = (bf16[24,8192]{1,0:T(8,128)(2,1)S(1)}, bf16[24,8192]{1,0:T(8,128)(2,1)S(1)}, u32[]{:S(2)}, u32[]{:S(2)}) collective-permute-start(bf16[24,8192]{1,0:T(8,128)(2,1)S(1)} %collective-permute-done), channel_id=1, source_target_pairs={{0,8},{2,10},{4,12},{6,14},{8,0},{10,2},{12,4},{14,6},{1,9},{3,11}... | collective-permute-start | bytes 1179656 | tf_op jit(solution)/shard_map/ppermute | solution.py:19
  41.6 17.7 %collective-permute-start.3 = (bf16[24,8192]{1,0:T(8,128)(2,1)S(1)}, bf16[24,8192]{1,0:T(8,128)(2,1)S(1)}, u32[]{:S(2)}, u32[]{:S(2)}) collective-permute-start(bf16[24,8192]{1,0:T(8,128)(2,1)S(1)} %collective-permute-done), channel_id=1, source_target_pairs={{0,12},{2,14},{4,0},{6,2},{8,4},{10,6},{12,8},{14,10},{1,13},{3,15... | collective-permute-start | bytes 1179656 | tf_op jit(solution)/shard_map/ppermute | solution.py:19
  59.3 13.7 %collective-permute-start.4 = (bf16[96,8192]{1,0:T(8,128)(2,1)S(1)}, bf16[96,8192]{1,0:T(8,128)(2,1)S(1)}, u32[]{:S(2)}, u32[]{:S(2)}) collective-permute-start(bf16[96,8192]{1,0:T(8,128)(2,1)S(1)} %constant_dynamic-update-slice_fusion.lhs_ref), channel_id=1, source_target_pairs={{0,2},{2,0},{4,6},{6,4},{8,10},{10,8},{12,14},{14,12},{1,3},{3,1},... | collective-permute-start | bytes 4718600 | tf_op jit(solution)/shard_map/ppermute | solution.py:24
  61.3 3.4 %copy-start = (bf16[8192,512]{1,0:T(8,128)(2,1)S(1)}, bf16[8192,512]{1,0:T(8,128)(2,1)}, u32[]{:S(2)}) copy-start(bf16[8192,512]{1,0:T(8,128)(2,1)} %w_ref.7) | copy-start | bytes 25165828
  64.6 3.4 %copy-start.1 = (bf16[8192,512]{1,0:T(8,128)(2,1)S(1)}, bf16[8192,512]{1,0:T(8,128)(2,1)}, u32[]{:S(2)}) copy-start(bf16[8192,512]{1,0:T(8,128)(2,1)} %w_ref.7) | copy-start | bytes 25165828
  73.0 8.2 %copy-start.5 = (s32[24,1]{0,1:T(1,128)S(1)}, s32[24,1]{0,1:T(1,128)}, u32[]{:S(2)}) copy-start(s32[24,1]{0,1:T(1,128)} %param.9) | copy-start | bytes 292
  76.2 20.0 %all-to-all-start = ((bf16[16,24,512]{2,1,0:T(8,128)(2,1)}), bf16[16,24,512]{2,1,0:T(8,128)(2,1)S(1)}, u32[]{:S(2)}, u32[]{:S(2)}) async-start(bf16[16,24,512]{2,1,0:T(8,128)(2,1)} %project.7), calls=%async_computation | async-start | bytes 786432 | tf_op jit(solution)/shard_map/all_to_all | solution.py:171
  99.2 19.2 %copy-start.3 = (bf16[8192]{0:T(1024)(128)(2,1)S(1)}, bf16[8192]{0:T(1024)(128)(2,1)}, u32[]{:S(2)}) copy-start(bf16[8192]{0:T(1024)(128)(2,1)} %param.11) | copy-start | bytes 49156
  99.2 78.2 %all-to-all-start.1 = ((bf16[48,2,8192]{2,1,0:T(2,128)(2,1)}), bf16[48,2,8192]{2,1,0:T(2,128)(2,1)}, u32[]{:S(2)}, u32[]{:S(2)}) async-start(bf16[48,2,8192]{2,1,0:T(2,128)(2,1)} %reshape.6), calls=%async_computation.1 | async-start | bytes 3145728 | tf_op jit(solution)/shard_map/all_to_all | solution.py:173
  118.4 61.5 %copy-start.2 = (bf16[96,8192]{1,0:T(8,128)(2,1)S(1)}, bf16[96,8192]{1,0:T(8,128)(2,1)}, u32[]{:S(2)}) copy-start(bf16[96,8192]{1,0:T(8,128)(2,1)} %text_ref.1) | copy-start | bytes 4718596
where the time goes:
time: 183 us; the launch traced here: 182 us
  waiting for transfers between devices  100 us (55%)
  starting transfers between devices  57.6 us (31%)
  Pallas kernels  13.8 us (8%)
  local copies, waits for them, and re-layouts  10.3 us (6%)
    all_to_all x1, waiting for transfers between devices, per_device(): lax.all_to_all(outbox.reshape(replicas, capacity, width), 'dp', split_axi...  58.9 us
    ppermute x6, waiting for transfers between devices, shift_x(): return lax.ppermute(block, 'section', pairs)  26.5 us
    ppermute x6, starting transfers between devices, shift_x(): return lax.ppermute(block, 'section', pairs)  22.8 us
    all_to_all x1, starting transfers between devices, per_device(): lax.all_to_all(outbox.reshape(replicas, capacity, width), 'dp', split_axi...  19.2 us
    all_to_all x1, waiting for transfers between devices, per_device(): lax.all_to_all(blocks, ('section', 'tensor'), split_axis=0, concat_axis=0...  15 us
    pallas_call x4, Pallas kernels, project(): pl.pallas_call(functools.partial(project_kernel, partner, swapped), in_sp...  10.7 us
    ppermute x1, starting transfers between devices, per_device(): partner = lax.ppermute(hidden, 'tensor', [(0, 1), (1, 0)])  6.82 us
    unnamed x19, local copies, waits for them, and re-layouts  5.47 us
  transfers between devices with their start and end apart: 11, of which 8 were waited for; matrix products, arithmetic and copies ran while one was open for 1% of the time, Pallas kernels for 4%

commit v1 on v0

--- a/solution.py
+++ b/solution.py
@@ -71,7 +71,8 @@
 
 def pack_kernel(route_ref, tokens_ref, out_ref):
     blocks, rows, width = tokens_ref.shape
-    slots = out_ref.shape[0]
+    replicas, capacity, _ = out_ref.shape
+    slots = replicas * capacity
     first = lax.broadcasted_iota(jnp.int32, (rows, rows), 0)
     second = lax.broadcasted_iota(jnp.int32, (rows, rows), 1)
     down = route_ref[...].astype(jnp.float32)
@@ -84,16 +85,18 @@
     pick = pick.astype(jnp.bfloat16)
     for k in range(blocks):
         moved = jnp.dot(pick, tokens_ref[k], preferred_element_type=jnp.float32)
-        out_ref[:, k * width : (k + 1) * width] = (moved + mark).astype(out_ref.dtype)
+        moved = (moved + mark).astype(out_ref.dtype)
+        out_ref[:, :, k * width : (k + 1) * width] = moved.reshape(replicas, capacity, width)
 
 
-def pack(route, tokens, slots):
+def pack(route, tokens, replicas, capacity):
     blocks, rows, width = tokens.shape
+    slots = replicas * capacity
     return pl.pallas_call(
         pack_kernel,
         in_specs=[pl.BlockSpec(memory_space=pltpu.VMEM)] * 2,
         out_specs=pl.BlockSpec(memory_space=pltpu.VMEM),
-        out_shape=jax.ShapeDtypeStruct((slots, blocks * width), jnp.bfloat16),
+        out_shape=jax.ShapeDtypeStruct((replicas, capacity, blocks * width), jnp.bfloat16),
         cost_estimate=pl.CostEstimate(
             flops=2 * slots * rows * blocks * width,
             bytes_accessed=2 * (slots + rows) * blocks * width,
@@ -105,11 +108,12 @@
 
 
 def finish_kernel(inbox_ref, text_ref, gain_ref, out_ref, merged):
-    slots, width = inbox_ref.shape
+    slots, width = inbox_ref.shape[0] * inbox_ref.shape[1], inbox_ref.shape[2]
     rows = text_ref.shape[0]
     first = lax.broadcasted_iota(jnp.int32, (slots, slots), 0)
     second = lax.broadcasted_iota(jnp.int32, (slots, slots), 1)
-    down = jnp.where(inbox_ref[:, 0:128].astype(jnp.float32)[:, 0:1] < EMPTY / 2, 1.0, 0.0)
+    head = inbox_ref[:, :, 0:128].reshape(slots, 128).astype(jnp.float32)
+    down = jnp.where(head[:, 0:1] < EMPTY / 2, 1.0, 0.0)
     across = jnp.sum(jnp.where(first == second, down, 0.0), axis=0, keepdims=True)
     place = jnp.sum(jnp.where(first < second, down, 0.0), axis=0, keepdims=True)
     ids = lax.broadcasted_iota(jnp.int32, (rows, slots), 0).astype(jnp.float32)
@@ -120,7 +124,8 @@
     square = jnp.zeros((rows, 1), jnp.float32)
     for k in range(width // step):
         at = slice(k * step, (k + 1) * step)
-        moved = jnp.dot(pick, inbox_ref[:, at], preferred_element_type=jnp.float32)
+        arrived = inbox_ref[:, :, at].reshape(slots, step)
+        moved = jnp.dot(pick, arrived, preferred_element_type=jnp.float32)
         values = jnp.where(is_image, moved, text_ref[:, at].astype(jnp.float32))
         merged[:, at] = values
         square += jnp.sum(values * values, axis=1, keepdims=True)
@@ -140,8 +145,8 @@
         out_shape=jax.ShapeDtypeStruct((rows, width), jnp.bfloat16),
         scratch_shapes=[pltpu.VMEM((rows, width), jnp.float32)],
         cost_estimate=pl.CostEstimate(
-            flops=2 * rows * inbox.shape[0] * width,
-            bytes_accessed=2 * (2 * rows + inbox.shape[0]) * width,
+            flops=4 * rows * inbox.shape[0] * width,
+            bytes_accessed=2 * (2 * rows + 2 * inbox.shape[0]) * width,
             transcendentals=rows,
         ),
         compiler_params=pltpu.CompilerParams(vmem_limit_bytes=GRANT),
@@ -151,7 +156,6 @@
 
 def per_device(hidden, proj_weight, proj_bias, route, text, norm_gain):
     replicas = lax.axis_size("dp")
-    _, width = hidden.shape
     capacity = 2
     bias = proj_bias[None, :]
     partner = lax.ppermute(hidden, "tensor", [(0, 1), (1, 0)])
@@ -169,11 +173,11 @@
         theirs = swap_core(mine)
         blocks = project(theirs, proj_weight, bias, name == "other", True, blocks)
     own = lax.all_to_all(blocks, ("section", "tensor"), split_axis=0, concat_axis=0, tiled=True)
-    outbox = pack(route, own, replicas * capacity)
+    outbox = pack(route, own, replicas, capacity)
     inbox = lax.all_to_all(
-        outbox.reshape(replicas, capacity, width), "dp", split_axis=0, concat_axis=0, tiled=True
+        outbox, "dp", split_axis=0, concat_axis=0, tiled=True
     )
-    return finish(inbox.reshape(replicas * capacity, width), text, norm_gain[None, :])
+    return finish(inbox, text, norm_gain[None, :])
 
 
 def solution(mesh):

time: 183 us -> 180 us (0.984)
  local copies, waits for them, and re-layouts: 10.3 us -> 5.54 us
    reshape x2 -> x0, local copies, waits for them, and re-layouts: 4.77 us -> none  [the longest x1 2.49 us: per_device(): inbox.reshape(replicas * capacity, width)]
where the time goes in v1:
time: 180 us; the launch traced here: 179 us
  waiting for transfers between devices  100 us (56%)
  starting transfers between devices  57.5 us (32%)
  Pallas kernels  15.2 us (8%)
  local copies, waits for them, and re-layouts  5.54 us (3%)
    all_to_all x1, waiting for transfers between devices, per_device(): lax.all_to_all(outbox, 'dp', split_axis=0, concat_axis=0, tiled=True)  59 us
    ppermute x6, waiting for transfers between devices, shift_x(): return lax.ppermute(block, 'section', pairs)  26.5 us
    ppermute x6, starting transfers between devices, shift_x(): return lax.ppermute(block, 'section', pairs)  22.8 us
    all_to_all x1, starting transfers between devices, per_device(): lax.all_to_all(outbox, 'dp', split_axis=0, concat_axis=0, tiled=True)  19.1 us
    all_to_all x1, waiting for transfers between devices, per_device(): lax.all_to_all(blocks, ('section', 'tensor'), split_axis=0, concat_axis=0...  15 us
    pallas_call x4, Pallas kernels, project(): pl.pallas_call(functools.partial(project_kernel, partner, swapped), in_sp...  10.7 us
    ppermute x1, starting transfers between devices, per_device(): partner = lax.ppermute(hidden, 'tensor', [(0, 1), (1, 0)])  6.82 us
    unnamed x19, local copies, waits for them, and re-layouts  5.47 us
  transfers between devices with their start and end apart: 11, of which 8 were waited for; matrix products, arithmetic and copies ran while one was open for 1% of the time, Pallas kernels for 4%

profile of v1, /device:TPU:8, one launch (start us, length us, event | category | flops | bytes accessed | tf_op | source)
XLA Modules:
  0.0 178.9 jit_solution(4767157451484220286)
XLA Ops:
  0.0 6.8 %collective-permute-start = (bf16[24,8192]{1,0:T(8,128)(2,1)}, bf16[24,8192]{1,0:T(8,128)(2,1)S(1)}, u32[]{:S(2)}, u32[]{:S(2)}) collective-permute-start(bf16[24,8192]{1,0:T(8,128)(2,1)} %param.6), channel_id=1, source_target_pairs={{0,1},{1,0},{2,3},{3,2},{4,5},{5,4},{6,7},{7,6},{8,9},{9,8},{10,11... | collective-permute-start | bytes 1179656 | tf_op jit(solution)/shard_map/ppermute | solution.py:161
  6.8 3.4 %collective-permute-start.5 = (bf16[24,8192]{1,0:T(8,128)(2,1)}, bf16[24,8192]{1,0:T(8,128)(2,1)S(1)}, u32[]{:S(2)}, u32[]{:S(2)}) collective-permute-start(bf16[24,8192]{1,0:T(8,128)(2,1)} %param.6), channel_id=1, source_target_pairs={{0,4},{2,6},{4,8},{6,10},{8,12},{10,14},{12,0},{14,2},{1,5},{3,7},... | collective-permute-start | bytes 1179656 | tf_op jit(solution)/shard_map/ppermute | solution.py:19
  10.2 4.6 %collective-permute-start.6 = (bf16[24,8192]{1,0:T(8,128)(2,1)}, bf16[24,8192]{1,0:T(8,128)(2,1)S(1)}, u32[]{:S(2)}, u32[]{:S(2)}) collective-permute-start(bf16[24,8192]{1,0:T(8,128)(2,1)} %param.6), channel_id=1, source_target_pairs={{0,8},{2,10},{4,12},{6,14},{8,0},{10,2},{12,4},{14,6},{1,9},{3,11}... | collective-permute-start | bytes 1179656 | tf_op jit(solution)/shard_map/ppermute | solution.py:19
  14.9 3.3 %collective-permute-start.7 = (bf16[24,8192]{1,0:T(8,128)(2,1)}, bf16[24,8192]{1,0:T(8,128)(2,1)S(1)}, u32[]{:S(2)}, u32[]{:S(2)}) collective-permute-start(bf16[24,8192]{1,0:T(8,128)(2,1)} %param.6), channel_id=1, source_target_pairs={{0,12},{2,14},{4,0},{6,2},{8,4},{10,6},{12,8},{14,10},{1,13},{3,15... | collective-permute-start | bytes 1179656 | tf_op jit(solution)/shard_map/ppermute | solution.py:19
  18.2 1.0 constant_dynamic-update-slice_fusion.7
  19.3 1.9 %collective-permute-done.5 = bf16[24,8192]{1,0:T(8,128)(2,1)S(1)} collective-permute-done((bf16[24,8192]{1,0:T(8,128)(2,1)}, bf16[24,8192]{1,0:T(8,128)(2,1)S(1)}, u32[]{:S(2)}, u32[]{:S(2)}) %collective-permute-start.5) | collective-permute-done | bytes 393248 | tf_op jit(solution)/shard_map/ppermute | solution.py:19
  21.2 9.0 %collective-permute-done.6 = bf16[24,8192]{1,0:T(8,128)(2,1)S(1)} collective-permute-done((bf16[24,8192]{1,0:T(8,128)(2,1)}, bf16[24,8192]{1,0:T(8,128)(2,1)S(1)}, u32[]{:S(2)}, u32[]{:S(2)}) %collective-permute-start.6) | collective-permute-done | bytes 393248 | tf_op jit(solution)/shard_map/ppermute | solution.py:19
  30.2 1.5 collective-permute-done.7
  31.7 0.0 copy-start.4
  31.7 1.9 %collective-permute-start.8 = (bf16[96,8192]{1,0:T(8,128)(2,1)S(1)}, bf16[96,8192]{1,0:T(8,128)(2,1)S(1)}, u32[]{:S(2)}, u32[]{:S(2)}) collective-permute-start(bf16[96,8192]{1,0:T(8,128)(2,1)S(1)} %constant_dynamic-update-slice_fusion.4.lhs_ref), channel_id=1, source_target_pairs={{0,2},{2,0},{4,6},{6,4},{8,10},{10,8},{12,14},{14,12},{1,3},{3,1},... | collective-permute-start | bytes 4718600 | tf_op jit(solution)/shard_map/ppermute | solution.py:24
  33.7 0.0 collective-permute-done
  33.7 4.3 %collective-permute-start.1 = (bf16[24,8192]{1,0:T(8,128)(2,1)S(1)}, bf16[24,8192]{1,0:T(8,128)(2,1)S(1)}, u32[]{:S(2)}, u32[]{:S(2)}) collective-permute-start(bf16[24,8192]{1,0:T(8,128)(2,1)S(1)} %collective-permute-done), channel_id=1, source_target_pairs={{0,4},{2,6},{4,8},{6,10},{8,12},{10,14},{12,0},{14,2},{1,5},{3,7},... | collective-permute-start | bytes 1179656 | tf_op jit(solution)/shard_map/ppermute | solution.py:19
  38.0 3.6 %collective-permute-start.2 = (bf16[24,8192]{1,0:T(8,128)(2,1)S(1)}, bf16[24,8192]{1,0:T(8,128)(2,1)S(1)}, u32[]{:S(2)}, u32[]{:S(2)}) collective-permute-start(bf16[24,8192]{1,0:T(8,128)(2,1)S(1)} %collective-permute-done), channel_id=1, source_target_pairs={{0,8},{2,10},{4,12},{6,14},{8,0},{10,2},{12,4},{14,6},{1,9},{3,11}... | collective-permute-start | bytes 1179656 | tf_op jit(solution)/shard_map/ppermute | solution.py:19
  41.6 3.5 %collective-permute-start.3 = (bf16[24,8192]{1,0:T(8,128)(2,1)S(1)}, bf16[24,8192]{1,0:T(8,128)(2,1)S(1)}, u32[]{:S(2)}, u32[]{:S(2)}) collective-permute-start(bf16[24,8192]{1,0:T(8,128)(2,1)S(1)} %collective-permute-done), channel_id=1, source_target_pairs={{0,12},{2,14},{4,0},{6,2},{8,4},{10,6},{12,8},{14,10},{1,13},{3,15... | collective-permute-start | bytes 1179656 | tf_op jit(solution)/shard_map/ppermute | solution.py:19
  45.1 3.2 %collective-permute-done.1 = bf16[24,8192]{1,0:T(8,128)(2,1)S(1)} collective-permute-done((bf16[24,8192]{1,0:T(8,128)(2,1)S(1)}, bf16[24,8192]{1,0:T(8,128)(2,1)S(1)}, u32[]{:S(2)}, u32[]{:S(2)}) %collective-permute-start.1) | collective-permute-done | bytes 393248 | tf_op jit(solution)/shard_map/ppermute | solution.py:19
  48.3 9.3 %collective-permute-done.2 = bf16[24,8192]{1,0:T(8,128)(2,1)S(1)} collective-permute-done((bf16[24,8192]{1,0:T(8,128)(2,1)S(1)}, bf16[24,8192]{1,0:T(8,128)(2,1)S(1)}, u32[]{:S(2)}, u32[]{:S(2)}) %collective-permute-start.2) | collective-permute-done | bytes 393248 | tf_op jit(solution)/shard_map/ppermute | solution.py:19
  57.6 1.7 collective-permute-done.3
  59.3 1.9 %collective-permute-start.4 = (bf16[96,8192]{1,0:T(8,128)(2,1)S(1)}, bf16[96,8192]{1,0:T(8,128)(2,1)S(1)}, u32[]{:S(2)}, u32[]{:S(2)}) collective-permute-start(bf16[96,8192]{1,0:T(8,128)(2,1)S(1)} %constant_dynamic-update-slice_fusion.lhs_ref), channel_id=1, source_target_pairs={{0,2},{2,0},{4,6},{6,4},{8,10},{10,8},{12,14},{14,12},{1,3},{3,1},... | collective-permute-start | bytes 4718600 | tf_op jit(solution)/shard_map/ppermute | solution.py:24
  61.2 0.0 copy-done.4
  61.3 0.0 copy-start
  61.3 3.4 %copy-done = bf16[8192,512]{1,0:T(8,128)(2,1)S(1)} copy-done((bf16[8192,512]{1,0:T(8,128)(2,1)S(1)}, bf16[8192,512]{1,0:T(8,128)(2,1)}, u32[]{:S(2)}) %copy-start) | copy-done | bytes 8388632
  64.6 0.0 copy-start.1
  64.7 2.5 %project.4.rest_0_ = bf16[16,24,512]{2,1,0:T(8,128)(2,1)S(1)} custom-call(bf16[96,8192]{1,0:T(8,128)(2,1)S(1)} %constant_dynamic-update-slice_fusion.4.lhs_ref, bf16[8192,512]{1,0:T(8,128)(2,1)S(1)} %copy-done, bf16[1,512]{1,0:T(2,128)(2,1)S(1)} %broadcast_in_dim.6.bias_ref), custom_call_target="tpu_custom_call" | custom-call | flops 805306368 | bytes 10059776 | tf_op jit(solution)/shard_map/project/pallas_call | solution.py:56
  67.2 0.0 collective-permute-done.8.lhs_ref
  67.2 0.8 copy-done.1
  68.0 2.5 %project.5.rest_0_ = bf16[16,24,512]{2,1,0:T(8,128)(2,1)S(1)} custom-call(bf16[96,8192]{1,0:T(8,128)(2,1)S(1)} %collective-permute-done.8.lhs_ref, bf16[8192,512]{1,0:T(8,128)(2,1)S(1)} %copy-done.1, bf16[1,512]{1,0:T(2,128)(2,1)S(1)} %broadcast_in_dim.6.bias_ref, bf16[16,24,512]{2,1,0:T(8,128)(2,1)S(1)} %project.4.rest_0_), custom_call_target="tpu_custom_call" | custom-call | flops 805306368 | bytes 10059776 | tf_op jit(solution)/shard_map/project/pallas_call | solution.py:56
  70.5 2.5 %project.6.rest_0_ = bf16[16,24,512]{2,1,0:T(8,128)(2,1)S(1)} custom-call(bf16[96,8192]{1,0:T(8,128)(2,1)S(1)} %constant_dynamic-update-slice_fusion.lhs_ref, bf16[8192,512]{1,0:T(8,128)(2,1)S(1)} %copy-done.1, bf16[1,512]{1,0:T(2,128)(2,1)S(1)} %broadcast_in_dim.6.bias_ref, bf16[16,24,512]{2,1,0:T(8,128)(2,1)S(1)} %project.5.rest_0_), custom_call_target="tpu_custom_call" | custom-call | flops 805306368 | bytes 10059776 | tf_op jit(solution)/shard_map/project/pallas_call | solution.py:56
  73.0 0.0 copy-start.5
  73.0 0.0 collective-permute-done.4.lhs_ref
  73.0 3.2 %project.7 = bf16[16,24,512]{2,1,0:T(8,128)(2,1)} custom-call(bf16[96,8192]{1,0:T(8,128)(2,1)S(1)} %collective-permute-done.4.lhs_ref, bf16[8192,512]{1,0:T(8,128)(2,1)S(1)} %copy-done.1, bf16[1,512]{1,0:T(2,128)(2,1)S(1)} %broadcast_in_dim.6.bias_ref, bf16[16,24,512]{2,1,0:T(8,128)(2,1)S(1)} %project.6.rest_0_), custom_call_target="tpu_custom_call" | custom-call | flops 805306368 | bytes 10059776 | tf_op jit(solution)/shard_map/project/pallas_call | solution.py:56
  76.2 4.9 %all-to-all-start = ((bf16[16,24,512]{2,1,0:T(8,128)(2,1)}), bf16[16,24,512]{2,1,0:T(8,128)(2,1)S(1)}, u32[]{:S(2)}, u32[]{:S(2)}) async-start(bf16[16,24,512]{2,1,0:T(8,128)(2,1)} %project.7), calls=%async_computation | async-start | bytes 786432 | tf_op jit(solution)/shard_map/all_to_all | solution.py:175
  81.2 0.0 copy-done.5
  81.2 0.1 copy.7.route_ref
  81.3 15.0 %all-to-all-done.tokens_ref = bf16[16,24,512]{2,1,0:T(8,128)(2,1)S(1)} async-done(((bf16[16,24,512]{2,1,0:T(8,128)(2,1)}), bf16[16,24,512]{2,1,0:T(8,128)(2,1)S(1)}, u32[]{:S(2)}, u32[]{:S(2)}) %all-to-all-start) | async-done | bytes 393248 | tf_op jit(solution)/shard_map/all_to_all | solution.py:175
  96.3 1.8 %pack.1 = bf16[48,2,8192]{2,1,0:T(2,128)(2,1)} custom-call(s32[24,1]{1,0:T(8,128)S(1)} %copy.7.route_ref, bf16[16,24,512]{2,1,0:T(8,128)(2,1)S(1)} %all-to-all-done.tokens_ref), custom_call_target="tpu_custom_call" | custom-call | flops 37748736 | bytes 1966080 | tf_op jit(solution)/shard_map/pack/pallas_call | solution.py:95
  98.1 0.0 copy-start.3
  98.1 0.0 copy-start.2
  98.1 19.1 %all-to-all-start.1 = ((bf16[48,2,8192]{2,1,0:T(2,128)(2,1)}), bf16[48,2,8192]{2,1,0:T(2,128)(2,1)S(1)}, u32[]{:S(2)}, u32[]{:S(2)}) async-start(bf16[48,2,8192]{2,1,0:T(2,128)(2,1)} %pack.1), calls=%async_computation.1 | async-start | bytes 3145728 | tf_op jit(solution)/shard_map/all_to_all | solution.py:177
  117.2 0.0 copy-done.3
  117.2 59.0 %all-to-all-done.1.inbox_ref = bf16[48,2,8192]{2,1,0:T(2,128)(2,1)S(1)} async-done(((bf16[48,2,8192]{2,1,0:T(2,128)(2,1)}), bf16[48,2,8192]{2,1,0:T(2,128)(2,1)S(1)}, u32[]{:S(2)}, u32[]{:S(2)}) %all-to-all-start.1) | async-done | bytes 1572896 | tf_op jit(solution)/shard_map/all_to_all | solution.py:177
  176.2 0.0 copy-done.2
  176.2 2.7 %finish.1 = bf16[96,8192]{1,0:T(8,128)(2,1)} custom-call(bf16[48,2,8192]{2,1,0:T(2,128)(2,1)S(1)} %all-to-all-done.1.inbox_ref, bf16[96,8192]{1,0:T(8,128)(2,1)S(1)} %copy-done.2, bf16[1,8192]{1,0:T(2,128)(2,1)S(1)} %broadcast_in_dim.7.gain_ref), custom_call_target="tpu_custom_call" | custom-call | flops 150994944 | bytes 4718592 | tf_op jit(solution)/shard_map/finish/pallas_call | solution.py:141
  (9 shorter events, 0.2 us)
Async XLA Ops:
  0.0 33.7 %collective-permute-start = (bf16[24,8192]{1,0:T(8,128)(2,1)}, bf16[24,8192]{1,0:T(8,128)(2,1)S(1)}, u32[]{:S(2)}, u32[]{:S(2)}) collective-permute-start(bf16[24,8192]{1,0:T(8,128)(2,1)} %param.6), channel_id=1, source_target_pairs={{0,1},{1,0},{2,3},{3,2},{4,5},{5,4},{6,7},{7,6},{8,9},{9,8},{10,11... | collective-permute-start | bytes 1179656 | tf_op jit(solution)/shard_map/ppermute | solution.py:161
  6.8 14.3 %collective-permute-start.5 = (bf16[24,8192]{1,0:T(8,128)(2,1)}, bf16[24,8192]{1,0:T(8,128)(2,1)S(1)}, u32[]{:S(2)}, u32[]{:S(2)}) collective-permute-start(bf16[24,8192]{1,0:T(8,128)(2,1)} %param.6), channel_id=1, source_target_pairs={{0,4},{2,6},{4,8},{6,10},{8,12},{10,14},{12,0},{14,2},{1,5},{3,7},... | collective-permute-start | bytes 1179656 | tf_op jit(solution)/shard_map/ppermute | solution.py:19
  10.2 19.9 %collective-permute-start.6 = (bf16[24,8192]{1,0:T(8,128)(2,1)}, bf16[24,8192]{1,0:T(8,128)(2,1)S(1)}, u32[]{:S(2)}, u32[]{:S(2)}) collective-permute-start(bf16[24,8192]{1,0:T(8,128)(2,1)} %param.6), channel_id=1, source_target_pairs={{0,8},{2,10},{4,12},{6,14},{8,0},{10,2},{12,4},{14,6},{1,9},{3,11}... | collective-permute-start | bytes 1179656 | tf_op jit(solution)/shard_map/ppermute | solution.py:19
  14.9 16.8 %collective-permute-start.7 = (bf16[24,8192]{1,0:T(8,128)(2,1)}, bf16[24,8192]{1,0:T(8,128)(2,1)S(1)}, u32[]{:S(2)}, u32[]{:S(2)}) collective-permute-start(bf16[24,8192]{1,0:T(8,128)(2,1)} %param.6), channel_id=1, source_target_pairs={{0,12},{2,14},{4,0},{6,2},{8,4},{10,6},{12,8},{14,10},{1,13},{3,15... | collective-permute-start | bytes 1179656 | tf_op jit(solution)/shard_map/ppermute | solution.py:19
  31.7 29.5 %copy-start.4 = (bf16[512]{0:T(512)(128)(2,1)S(1)}, bf16[512]{0:T(512)(128)(2,1)}, u32[]{:S(2)}) copy-start(bf16[512]{0:T(512)(128)(2,1)} %param.8) | copy-start | bytes 3076
  31.7 35.5 %collective-permute-start.8 = (bf16[96,8192]{1,0:T(8,128)(2,1)S(1)}, bf16[96,8192]{1,0:T(8,128)(2,1)S(1)}, u32[]{:S(2)}, u32[]{:S(2)}) collective-permute-start(bf16[96,8192]{1,0:T(8,128)(2,1)S(1)} %constant_dynamic-update-slice_fusion.4.lhs_ref), channel_id=1, source_target_pairs={{0,2},{2,0},{4,6},{6,4},{8,10},{10,8},{12,14},{14,12},{1,3},{3,1},... | collective-permute-start | bytes 4718600 | tf_op jit(solution)/shard_map/ppermute | solution.py:24
  33.7 14.6 %collective-permute-start.1 = (bf16[24,8192]{1,0:T(8,128)(2,1)S(1)}, bf16[24,8192]{1,0:T(8,128)(2,1)S(1)}, u32[]{:S(2)}, u32[]{:S(2)}) collective-permute-start(bf16[24,8192]{1,0:T(8,128)(2,1)S(1)} %collective-permute-done), channel_id=1, source_target_pairs={{0,4},{2,6},{4,8},{6,10},{8,12},{10,14},{12,0},{14,2},{1,5},{3,7},... | collective-permute-start | bytes 1179656 | tf_op jit(solution)/shard_map/ppermute | solution.py:19
  38.0 19.6 %collective-permute-start.2 = (bf16[24,8192]{1,0:T(8,128)(2,1)S(1)}, bf16[24,8192]{1,0:T(8,128)(2,1)S(1)}, u32[]{:S(2)}, u32[]{:S(2)}) collective-permute-start(bf16[24,8192]{1,0:T(8,128)(2,1)S(1)} %collective-permute-done), channel_id=1, source_target_pairs={{0,8},{2,10},{4,12},{6,14},{8,0},{10,2},{12,4},{14,6},{1,9},{3,11}... | collective-permute-start | bytes 1179656 | tf_op jit(solution)/shard_map/ppermute | solution.py:19
  41.6 17.7 %collective-permute-start.3 = (bf16[24,8192]{1,0:T(8,128)(2,1)S(1)}, bf16[24,8192]{1,0:T(8,128)(2,1)S(1)}, u32[]{:S(2)}, u32[]{:S(2)}) collective-permute-start(bf16[24,8192]{1,0:T(8,128)(2,1)S(1)} %collective-permute-done), channel_id=1, source_target_pairs={{0,12},{2,14},{4,0},{6,2},{8,4},{10,6},{12,8},{14,10},{1,13},{3,15... | collective-permute-start | bytes 1179656 | tf_op jit(solution)/shard_map/ppermute | solution.py:19
  59.3 13.7 %collective-permute-start.4 = (bf16[96,8192]{1,0:T(8,128)(2,1)S(1)}, bf16[96,8192]{1,0:T(8,128)(2,1)S(1)}, u32[]{:S(2)}, u32[]{:S(2)}) collective-permute-start(bf16[96,8192]{1,0:T(8,128)(2,1)S(1)} %constant_dynamic-update-slice_fusion.lhs_ref), channel_id=1, source_target_pairs={{0,2},{2,0},{4,6},{6,4},{8,10},{10,8},{12,14},{14,12},{1,3},{3,1},... | collective-permute-start | bytes 4718600 | tf_op jit(solution)/shard_map/ppermute | solution.py:24
  61.3 3.4 %copy-start = (bf16[8192,512]{1,0:T(8,128)(2,1)S(1)}, bf16[8192,512]{1,0:T(8,128)(2,1)}, u32[]{:S(2)}) copy-start(bf16[8192,512]{1,0:T(8,128)(2,1)} %w_ref.7) | copy-start | bytes 25165828
  64.6 3.4 %copy-start.1 = (bf16[8192,512]{1,0:T(8,128)(2,1)S(1)}, bf16[8192,512]{1,0:T(8,128)(2,1)}, u32[]{:S(2)}) copy-start(bf16[8192,512]{1,0:T(8,128)(2,1)} %w_ref.7) | copy-start | bytes 25165828
  73.0 8.2 %copy-start.5 = (s32[24,1]{0,1:T(1,128)S(1)}, s32[24,1]{0,1:T(1,128)}, u32[]{:S(2)}) copy-start(s32[24,1]{0,1:T(1,128)} %param.9) | copy-start | bytes 292
  76.2 20.0 %all-to-all-start = ((bf16[16,24,512]{2,1,0:T(8,128)(2,1)}), bf16[16,24,512]{2,1,0:T(8,128)(2,1)S(1)}, u32[]{:S(2)}, u32[]{:S(2)}) async-start(bf16[16,24,512]{2,1,0:T(8,128)(2,1)} %project.7), calls=%async_computation | async-start | bytes 786432 | tf_op jit(solution)/shard_map/all_to_all | solution.py:175
  98.1 19.1 %copy-start.3 = (bf16[8192]{0:T(1024)(128)(2,1)S(1)}, bf16[8192]{0:T(1024)(128)(2,1)}, u32[]{:S(2)}) copy-start(bf16[8192]{0:T(1024)(128)(2,1)} %param.11) | copy-start | bytes 49156
  98.1 78.1 %copy-start.2 = (bf16[96,8192]{1,0:T(8,128)(2,1)S(1)}, bf16[96,8192]{1,0:T(8,128)(2,1)}, u32[]{:S(2)}) copy-start(bf16[96,8192]{1,0:T(8,128)(2,1)} %text_ref.1) | copy-start | bytes 4718596
  98.1 78.1 %all-to-all-start.1 = ((bf16[48,2,8192]{2,1,0:T(2,128)(2,1)}), bf16[48,2,8192]{2,1,0:T(2,128)(2,1)S(1)}, u32[]{:S(2)}, u32[]{:S(2)}) async-start(bf16[48,2,8192]{2,1,0:T(2,128)(2,1)} %pack.1), calls=%async_computation.1 | async-start | bytes 3145728 | tf_op jit(solution)/shard_map/all_to_all | solution.py:177

commit v2 on v1

--- a/solution.py
+++ b/solution.py
@@ -8,7 +8,6 @@
 from jax.sharding import PartitionSpec as P
 
 
-EMPTY = 2.0**100
 NX = 4
 GRANT = 16 * 1024 * 1024
 
@@ -69,6 +68,30 @@
     )(*operands)
 
 
+def count_kernel(route_ref, out_ref):
+    rows = route_ref.shape[0]
+    replicas, _, lanes = out_ref.shape
+    first = lax.broadcasted_iota(jnp.int32, (rows, rows), 0)
+    second = lax.broadcasted_iota(jnp.int32, (rows, rows), 1)
+    down = route_ref[...].astype(jnp.float32)
+    across = jnp.sum(jnp.where(first == second, down, 0.0), axis=0, keepdims=True)
+    ids = lax.broadcasted_iota(jnp.int32, (replicas, rows), 0).astype(jnp.float32)
+    counts = jnp.sum(jnp.where(ids == across, 1.0, 0.0), axis=1, keepdims=True)
+    counts = jnp.broadcast_to(counts, (replicas, lanes)).astype(jnp.int32)
+    out_ref[...] = counts.reshape(replicas, 1, lanes)
+
+
+def count(route, replicas):
+    return pl.pallas_call(
+        count_kernel,
+        in_specs=[pl.BlockSpec(memory_space=pltpu.VMEM)],
+        out_specs=pl.BlockSpec(memory_space=pltpu.VMEM),
+        out_shape=jax.ShapeDtypeStruct((replicas, 1, 128), jnp.int32),
+        compiler_params=pltpu.CompilerParams(vmem_limit_bytes=GRANT),
+        name="count",
+    )(route)
+
+
 def pack_kernel(route_ref, tokens_ref, out_ref):
     blocks, rows, width = tokens_ref.shape
     replicas, capacity, _ = out_ref.shape
@@ -81,12 +104,11 @@
     slot = 2.0 * across + jnp.sum(earlier, axis=0, keepdims=True)
     ids = lax.broadcasted_iota(jnp.int32, (slots, rows), 0).astype(jnp.float32)
     pick = jnp.where(ids == slot, 1.0, 0.0)
-    mark = jnp.where(jnp.sum(pick, axis=1, keepdims=True) > 0.0, 0.0, EMPTY)
     pick = pick.astype(jnp.bfloat16)
     for k in range(blocks):
         moved = jnp.dot(pick, tokens_ref[k], preferred_element_type=jnp.float32)
-        moved = (moved + mark).astype(out_ref.dtype)
-        out_ref[:, :, k * width : (k + 1) * width] = moved.reshape(replicas, capacity, width)
+        moved = moved.astype(out_ref.dtype).reshape(replicas, capacity, width)
+        out_ref[:, :, k * width : (k + 1) * width] = moved
 
 
 def pack(route, tokens, replicas, capacity):
@@ -107,13 +129,22 @@
     )(route, tokens)
 
 
-def finish_kernel(inbox_ref, text_ref, gain_ref, out_ref, merged):
-    slots, width = inbox_ref.shape[0] * inbox_ref.shape[1], inbox_ref.shape[2]
+def finish_kernel(counts_ref, inbox_ref, text_ref, gain_ref, out_ref, merged):
+    replicas, capacity, width = inbox_ref.shape
+    slots = replicas * capacity
     rows = text_ref.shape[0]
     first = lax.broadcasted_iota(jnp.int32, (slots, slots), 0)
     second = lax.broadcasted_iota(jnp.int32, (slots, slots), 1)
-    head = inbox_ref[:, :, 0:128].reshape(slots, 128).astype(jnp.float32)
-    down = jnp.where(head[:, 0:1] < EMPTY / 2, 1.0, 0.0)
+    counts = counts_ref[...].reshape(replicas, 128).astype(jnp.float32)[:, 0:1]
+    same = lax.broadcasted_iota(jnp.int32, (replicas, replicas), 0) == (
+        lax.broadcasted_iota(jnp.int32, (replicas, replicas), 1)
+    )
+    counts = jnp.sum(jnp.where(same, counts, 0.0), axis=0, keepdims=True)
+    place_in = lax.broadcasted_iota(jnp.int32, (slots, replicas), 0) - (
+        capacity * lax.broadcasted_iota(jnp.int32, (slots, replicas), 1)
+    )
+    held = (place_in >= 0) & (place_in < capacity) & (place_in.astype(jnp.float32) < counts)
+    down = jnp.sum(jnp.where(held, 1.0, 0.0), axis=1, keepdims=True)
     across = jnp.sum(jnp.where(first == second, down, 0.0), axis=0, keepdims=True)
     place = jnp.sum(jnp.where(first < second, down, 0.0), axis=0, keepdims=True)
     ids = lax.broadcasted_iota(jnp.int32, (rows, slots), 0).astype(jnp.float32)
@@ -136,11 +167,11 @@
         out_ref[:, at] = (merged[:, at] * scale_inv * gain).astype(out_ref.dtype)
 
 
-def finish(inbox, text, gain):
+def finish(counts, inbox, text, gain):
     rows, width = text.shape
     return pl.pallas_call(
         finish_kernel,
-        in_specs=[pl.BlockSpec(memory_space=pltpu.VMEM)] * 3,
+        in_specs=[pl.BlockSpec(memory_space=pltpu.VMEM)] * 4,
         out_specs=pl.BlockSpec(memory_space=pltpu.VMEM),
         out_shape=jax.ShapeDtypeStruct((rows, width), jnp.bfloat16),
         scratch_shapes=[pltpu.VMEM((rows, width), jnp.float32)],
@@ -151,7 +182,7 @@
         ),
         compiler_params=pltpu.CompilerParams(vmem_limit_bytes=GRANT),
         name="finish",
-    )(inbox, text, gain)
+    )(counts, inbox, text, gain)
 
 
 def per_device(hidden, proj_weight, proj_bias, route, text, norm_gain):
@@ -159,6 +190,8 @@
     capacity = 2
     bias = proj_bias[None, :]
     partner = lax.ppermute(hidden, "tensor", [(0, 1), (1, 0)])
+
+    counts = lax.all_to_all(count(route, replicas), "dp", split_axis=0, concat_axis=0, tiled=True)
 
     def along_x(block):
         pieces = [block]
@@ -177,7 +210,7 @@
     inbox = lax.all_to_all(
         outbox, "dp", split_axis=0, concat_axis=0, tiled=True
     )
-    return finish(inbox, text, norm_gain[None, :])
+    return finish(counts, inbox, text, norm_gain[None, :])
 
 
 def solution(mesh):

time: 180 us -> 194 us (1.078)
  waiting for transfers between devices: 100 us -> 108 us
  starting transfers between devices: 57.5 us -> 63 us
    all_to_all x0 -> x1, starting transfers between devices: none -> 19 us  [per_device(): lax.all_to_all(count(route, replicas), 'dp', split_axis=0, concat_axis=0,...]
    all_to_all x1, starting transfers between devices: 19.1 us -> 5.68 us  [per_device(): lax.all_to_all(outbox, 'dp', split_axis=0, concat_axis=0, tiled=True)]
    all_to_all x0 -> x1, waiting for transfers between devices: none -> 9.7 us  [per_device(): lax.all_to_all(count(route, replicas), 'dp', split_axis=0, concat_axis=0,...]
  transfers between devices with their start and end apart: 11 -> 12, of which waited for: 8 -> 9; matrix products, arithmetic and copies ran while one was open for 1% -> 1% of each run, Pallas kernels for 4% -> 5%
where the time goes in v2:
time: 194 us; the launch traced here: 193 us
  waiting for transfers between devices  108 us (56%)
  starting transfers between devices  63 us (32%)
  Pallas kernels  16.1 us (8%)
  local copies, waits for them, and re-layouts  5.54 us (3%)
    all_to_all x1, waiting for transfers between devices, per_device(): lax.all_to_all(outbox, 'dp', split_axis=0, concat_axis=0, tiled=True)  57.8 us
    ppermute x6, waiting for transfers between devices, shift_x(): return lax.ppermute(block, 'section', pairs)  26.5 us
    ppermute x6, starting transfers between devices, shift_x(): return lax.ppermute(block, 'section', pairs)  22.8 us
    all_to_all x1, starting transfers between devices, per_device(): lax.all_to_all(count(route, replicas), 'dp', split_axis=0, concat_axis=0,...  19 us
    all_to_all x1, waiting for transfers between devices, per_device(): lax.all_to_all(blocks, ('section', 'tensor'), split_axis=0, concat_axis=0...  14.2 us
    pallas_call x4, Pallas kernels, project(): pl.pallas_call(functools.partial(project_kernel, partner, swapped), in_sp...  10.7 us
    all_to_all x1, waiting for transfers between devices, per_device(): lax.all_to_all(count(route, replicas), 'dp', split_axis=0, concat_axis=0,...  9.7 us
    ppermute x1, starting transfers between devices, per_device(): partner = lax.ppermute(hidden, 'tensor', [(0, 1), (1, 0)])  6.82 us
  transfers between devices with their start and end apart: 12, of which 9 were waited for; matrix products, arithmetic and copies ran while one was open for 1% of the time, Pallas kernels for 5%

profile of v2, /device:TPU:8, one launch (start us, length us, event | category | flops | bytes accessed | tf_op | source)
XLA Modules:
  0.0 193.1 jit_solution(8178364055884195608)
XLA Ops:
  0.0 6.8 %collective-permute-start = (bf16[24,8192]{1,0:T(8,128)(2,1)}, bf16[24,8192]{1,0:T(8,128)(2,1)S(1)}, u32[]{:S(2)}, u32[]{:S(2)}) collective-permute-start(bf16[24,8192]{1,0:T(8,128)(2,1)} %param.6), channel_id=1, source_target_pairs={{0,1},{1,0},{2,3},{3,2},{4,5},{5,4},{6,7},{7,6},{8,9},{9,8},{10,11... | collective-permute-start | bytes 1179656 | tf_op jit(solution)/shard_map/ppermute | solution.py:192
  6.8 3.4 %collective-permute-start.5 = (bf16[24,8192]{1,0:T(8,128)(2,1)}, bf16[24,8192]{1,0:T(8,128)(2,1)S(1)}, u32[]{:S(2)}, u32[]{:S(2)}) collective-permute-start(bf16[24,8192]{1,0:T(8,128)(2,1)} %param.6), channel_id=1, source_target_pairs={{0,4},{2,6},{4,8},{6,10},{8,12},{10,14},{12,0},{14,2},{1,5},{3,7},... | collective-permute-start | bytes 1179656 | tf_op jit(solution)/shard_map/ppermute | solution.py:18
  10.2 4.6 %collective-permute-start.6 = (bf16[24,8192]{1,0:T(8,128)(2,1)}, bf16[24,8192]{1,0:T(8,128)(2,1)S(1)}, u32[]{:S(2)}, u32[]{:S(2)}) collective-permute-start(bf16[24,8192]{1,0:T(8,128)(2,1)} %param.6), channel_id=1, source_target_pairs={{0,8},{2,10},{4,12},{6,14},{8,0},{10,2},{12,4},{14,6},{1,9},{3,11}... | collective-permute-start | bytes 1179656 | tf_op jit(solution)/shard_map/ppermute | solution.py:18
  14.9 3.3 %collective-permute-start.7 = (bf16[24,8192]{1,0:T(8,128)(2,1)}, bf16[24,8192]{1,0:T(8,128)(2,1)S(1)}, u32[]{:S(2)}, u32[]{:S(2)}) collective-permute-start(bf16[24,8192]{1,0:T(8,128)(2,1)} %param.6), channel_id=1, source_target_pairs={{0,12},{2,14},{4,0},{6,2},{8,4},{10,6},{12,8},{14,10},{1,13},{3,15... | collective-permute-start | bytes 1179656 | tf_op jit(solution)/shard_map/ppermute | solution.py:18
  18.2 1.0 constant_dynamic-update-slice_fusion.7
  19.3 1.9 collective-permute-done.5
  21.2 9.0 %collective-permute-done.6 = bf16[24,8192]{1,0:T(8,128)(2,1)S(1)} collective-permute-done((bf16[24,8192]{1,0:T(8,128)(2,1)}, bf16[24,8192]{1,0:T(8,128)(2,1)S(1)}, u32[]{:S(2)}, u32[]{:S(2)}) %collective-permute-start.6) | collective-permute-done | bytes 393248 | tf_op jit(solution)/shard_map/ppermute | solution.py:18
  30.2 1.5 collective-permute-done.7
  31.7 0.0 copy-start.4
  31.7 1.9 collective-permute-start.8
  33.7 0.0 collective-permute-done
  33.7 4.3 %collective-permute-start.1 = (bf16[24,8192]{1,0:T(8,128)(2,1)S(1)}, bf16[24,8192]{1,0:T(8,128)(2,1)S(1)}, u32[]{:S(2)}, u32[]{:S(2)}) collective-permute-start(bf16[24,8192]{1,0:T(8,128)(2,1)S(1)} %collective-permute-done), channel_id=1, source_target_pairs={{0,4},{2,6},{4,8},{6,10},{8,12},{10,14},{12,0},{14,2},{1,5},{3,7},... | collective-permute-start | bytes 1179656 | tf_op jit(solution)/shard_map/ppermute | solution.py:18
  38.0 3.6 %collective-permute-start.2 = (bf16[24,8192]{1,0:T(8,128)(2,1)S(1)}, bf16[24,8192]{1,0:T(8,128)(2,1)S(1)}, u32[]{:S(2)}, u32[]{:S(2)}) collective-permute-start(bf16[24,8192]{1,0:T(8,128)(2,1)S(1)} %collective-permute-done), channel_id=1, source_target_pairs={{0,8},{2,10},{4,12},{6,14},{8,0},{10,2},{12,4},{14,6},{1,9},{3,11}... | collective-permute-start | bytes 1179656 | tf_op jit(solution)/shard_map/ppermute | solution.py:18
  41.6 3.5 %collective-permute-start.3 = (bf16[24,8192]{1,0:T(8,128)(2,1)S(1)}, bf16[24,8192]{1,0:T(8,128)(2,1)S(1)}, u32[]{:S(2)}, u32[]{:S(2)}) collective-permute-start(bf16[24,8192]{1,0:T(8,128)(2,1)S(1)} %collective-permute-done), channel_id=1, source_target_pairs={{0,12},{2,14},{4,0},{6,2},{8,4},{10,6},{12,8},{14,10},{1,13},{3,15... | collective-permute-start | bytes 1179656 | tf_op jit(solution)/shard_map/ppermute | solution.py:18
  45.1 3.2 %collective-permute-done.1 = bf16[24,8192]{1,0:T(8,128)(2,1)S(1)} collective-permute-done((bf16[24,8192]{1,0:T(8,128)(2,1)S(1)}, bf16[24,8192]{1,0:T(8,128)(2,1)S(1)}, u32[]{:S(2)}, u32[]{:S(2)}) %collective-permute-start.1) | collective-permute-done | bytes 393248 | tf_op jit(solution)/shard_map/ppermute | solution.py:18
  48.3 9.3 %collective-permute-done.2 = bf16[24,8192]{1,0:T(8,128)(2,1)S(1)} collective-permute-done((bf16[24,8192]{1,0:T(8,128)(2,1)S(1)}, bf16[24,8192]{1,0:T(8,128)(2,1)S(1)}, u32[]{:S(2)}, u32[]{:S(2)}) %collective-permute-start.2) | collective-permute-done | bytes 393248 | tf_op jit(solution)/shard_map/ppermute | solution.py:18
  57.6 1.7 collective-permute-done.3
  59.3 1.9 collective-permute-start.4
  61.2 0.0 copy-done.4
  61.3 0.0 copy-start
  61.3 3.4 %copy-done = bf16[8192,512]{1,0:T(8,128)(2,1)S(1)} copy-done((bf16[8192,512]{1,0:T(8,128)(2,1)S(1)}, bf16[8192,512]{1,0:T(8,128)(2,1)}, u32[]{:S(2)}) %copy-start) | copy-done | bytes 8388632
  64.6 0.0 copy-start.1
  64.7 2.5 %project.4.rest_0_ = bf16[16,24,512]{2,1,0:T(8,128)(2,1)S(1)} custom-call(bf16[96,8192]{1,0:T(8,128)(2,1)S(1)} %constant_dynamic-update-slice_fusion.4.lhs_ref, bf16[8192,512]{1,0:T(8,128)(2,1)S(1)} %copy-done, bf16[1,512]{1,0:T(2,128)(2,1)S(1)} %broadcast_in_dim.6.bias_ref), custom_call_target="tpu_custom_call" | custom-call | flops 805306368 | bytes 10059776 | tf_op jit(solution)/shard_map/project/pallas_call | solution.py:55
  67.2 0.0 collective-permute-done.8.lhs_ref
  67.2 0.8 copy-done.1
  68.0 2.5 %project.5.rest_0_ = bf16[16,24,512]{2,1,0:T(8,128)(2,1)S(1)} custom-call(bf16[96,8192]{1,0:T(8,128)(2,1)S(1)} %collective-permute-done.8.lhs_ref, bf16[8192,512]{1,0:T(8,128)(2,1)S(1)} %copy-done.1, bf16[1,512]{1,0:T(2,128)(2,1)S(1)} %broadcast_in_dim.6.bias_ref, bf16[16,24,512]{2,1,0:T(8,128)(2,1)S(1)} %project.4.rest_0_), custom_call_target="tpu_custom_call" | custom-call | flops 805306368 | bytes 10059776 | tf_op jit(solution)/shard_map/project/pallas_call | solution.py:55
  70.5 2.5 %project.6.rest_0_ = bf16[16,24,512]{2,1,0:T(8,128)(2,1)S(1)} custom-call(bf16[96,8192]{1,0:T(8,128)(2,1)S(1)} %constant_dynamic-update-slice_fusion.lhs_ref, bf16[8192,512]{1,0:T(8,128)(2,1)S(1)} %copy-done.1, bf16[1,512]{1,0:T(2,128)(2,1)S(1)} %broadcast_in_dim.6.bias_ref, bf16[16,24,512]{2,1,0:T(8,128)(2,1)S(1)} %project.5.rest_0_), custom_call_target="tpu_custom_call" | custom-call | flops 805306368 | bytes 10059776 | tf_op jit(solution)/shard_map/project/pallas_call | solution.py:55
  73.0 0.0 copy-start.5
  73.0 0.0 collective-permute-done.4.lhs_ref
  73.0 3.2 %project.7 = bf16[16,24,512]{2,1,0:T(8,128)(2,1)} custom-call(bf16[96,8192]{1,0:T(8,128)(2,1)S(1)} %collective-permute-done.4.lhs_ref, bf16[8192,512]{1,0:T(8,128)(2,1)S(1)} %copy-done.1, bf16[1,512]{1,0:T(2,128)(2,1)S(1)} %broadcast_in_dim.6.bias_ref, bf16[16,24,512]{2,1,0:T(8,128)(2,1)S(1)} %project.6.rest_0_), custom_call_target="tpu_custom_call" | custom-call | flops 805306368 | bytes 10059776 | tf_op jit(solution)/shard_map/project/pallas_call | solution.py:55
  76.2 4.9 %all-to-all-start.1 = ((bf16[16,24,512]{2,1,0:T(8,128)(2,1)}), bf16[16,24,512]{2,1,0:T(8,128)(2,1)S(1)}, u32[]{:S(2)}, u32[]{:S(2)}) async-start(bf16[16,24,512]{2,1,0:T(8,128)(2,1)} %project.7), calls=%async_computation.1 | async-start | bytes 786432 | tf_op jit(solution)/shard_map/all_to_all | solution.py:208
  81.2 0.0 copy-done.5
  81.2 0.1 copy.7.route_ref
  81.3 0.8 count.1
  82.1 14.2 %all-to-all-done.1.tokens_ref = bf16[16,24,512]{2,1,0:T(8,128)(2,1)S(1)} async-done(((bf16[16,24,512]{2,1,0:T(8,128)(2,1)}), bf16[16,24,512]{2,1,0:T(8,128)(2,1)S(1)}, u32[]{:S(2)}, u32[]{:S(2)}) %all-to-all-start.1) | async-done | bytes 393248 | tf_op jit(solution)/shard_map/all_to_all | solution.py:208
  96.3 19.0 %all-to-all-start = ((s32[48,1,128]{2,1,0:T(1,128)}), s32[48,1,128]{2,1,0:T(1,128)S(1)}, u32[]{:S(2)}, u32[]{:S(2)}) async-start(s32[48,1,128]{2,1,0:T(1,128)} %count.1), calls=%async_computation | async-start | bytes 49152 | tf_op jit(solution)/shard_map/all_to_all | solution.py:194
  115.2 1.8 pack.1
  117.0 0.0 copy-start.3
  117.0 0.0 copy-start.2
  117.0 9.7 %all-to-all-done.counts_ref = s32[48,1,128]{2,1,0:T(1,128)S(1)} async-done(((s32[48,1,128]{2,1,0:T(1,128)}), s32[48,1,128]{2,1,0:T(1,128)S(1)}, u32[]{:S(2)}, u32[]{:S(2)}) %all-to-all-start) | async-done | bytes 24608 | tf_op jit(solution)/shard_map/all_to_all | solution.py:194
  126.7 5.7 %all-to-all-start.2 = ((bf16[48,2,8192]{2,1,0:T(2,128)(2,1)}), bf16[48,2,8192]{2,1,0:T(2,128)(2,1)S(1)}, u32[]{:S(2)}, u32[]{:S(2)}) async-start(bf16[48,2,8192]{2,1,0:T(2,128)(2,1)} %pack.1), calls=%async_computation.2 | async-start | bytes 3145728 | tf_op jit(solution)/shard_map/all_to_all | solution.py:210
  132.4 0.0 copy-done.3
  132.5 57.8 %all-to-all-done.2.inbox_ref = bf16[48,2,8192]{2,1,0:T(2,128)(2,1)S(1)} async-done(((bf16[48,2,8192]{2,1,0:T(2,128)(2,1)}), bf16[48,2,8192]{2,1,0:T(2,128)(2,1)S(1)}, u32[]{:S(2)}, u32[]{:S(2)}) %all-to-all-start.2) | async-done | bytes 1572896 | tf_op jit(solution)/shard_map/all_to_all | solution.py:210
  190.3 0.0 copy-done.2
  190.3 2.8 %finish.1 = bf16[96,8192]{1,0:T(8,128)(2,1)} custom-call(s32[48,1,128]{2,1,0:T(1,128)S(1)} %all-to-all-done.counts_ref, bf16[48,2,8192]{2,1,0:T(2,128)(2,1)S(1)} %all-to-all-done.2.inbox_ref, bf16[96,8192]{1,0:T(8,128)(2,1)S(1)} %copy-done.2, bf16[1,8192]{1,0:T(2,128)(2,1)S(1)} %broadcast_in_dim.7.gain_ref), custom_call_target="tpu_custom_call" | custom-call | flops 150994944 | bytes 4718592 | tf_op jit(solution)/shard_map/finish/pallas_call | solution.py:172
  (9 shorter events, 0.2 us)
Async XLA Ops:
  0.0 33.7 %collective-permute-start = (bf16[24,8192]{1,0:T(8,128)(2,1)}, bf16[24,8192]{1,0:T(8,128)(2,1)S(1)}, u32[]{:S(2)}, u32[]{:S(2)}) collective-permute-start(bf16[24,8192]{1,0:T(8,128)(2,1)} %param.6), channel_id=1, source_target_pairs={{0,1},{1,0},{2,3},{3,2},{4,5},{5,4},{6,7},{7,6},{8,9},{9,8},{10,11... | collective-permute-start | bytes 1179656 | tf_op jit(solution)/shard_map/ppermute | solution.py:192
  6.8 14.3 %collective-permute-start.5 = (bf16[24,8192]{1,0:T(8,128)(2,1)}, bf16[24,8192]{1,0:T(8,128)(2,1)S(1)}, u32[]{:S(2)}, u32[]{:S(2)}) collective-permute-start(bf16[24,8192]{1,0:T(8,128)(2,1)} %param.6), channel_id=1, source_target_pairs={{0,4},{2,6},{4,8},{6,10},{8,12},{10,14},{12,0},{14,2},{1,5},{3,7},... | collective-permute-start | bytes 1179656 | tf_op jit(solution)/shard_map/ppermute | solution.py:18
  10.2 19.9 %collective-permute-start.6 = (bf16[24,8192]{1,0:T(8,128)(2,1)}, bf16[24,8192]{1,0:T(8,128)(2,1)S(1)}, u32[]{:S(2)}, u32[]{:S(2)}) collective-permute-start(bf16[24,8192]{1,0:T(8,128)(2,1)} %param.6), channel_id=1, source_target_pairs={{0,8},{2,10},{4,12},{6,14},{8,0},{10,2},{12,4},{14,6},{1,9},{3,11}... | collective-permute-start | bytes 1179656 | tf_op jit(solution)/shard_map/ppermute | solution.py:18
  14.9 16.8 %collective-permute-start.7 = (bf16[24,8192]{1,0:T(8,128)(2,1)}, bf16[24,8192]{1,0:T(8,128)(2,1)S(1)}, u32[]{:S(2)}, u32[]{:S(2)}) collective-permute-start(bf16[24,8192]{1,0:T(8,128)(2,1)} %param.6), channel_id=1, source_target_pairs={{0,12},{2,14},{4,0},{6,2},{8,4},{10,6},{12,8},{14,10},{1,13},{3,15... | collective-permute-start | bytes 1179656 | tf_op jit(solution)/shard_map/ppermute | solution.py:18
  31.7 29.5 %copy-start.4 = (bf16[512]{0:T(512)(128)(2,1)S(1)}, bf16[512]{0:T(512)(128)(2,1)}, u32[]{:S(2)}) copy-start(bf16[512]{0:T(512)(128)(2,1)} %param.8) | copy-start | bytes 3076
  31.7 35.5 %collective-permute-start.8 = (bf16[96,8192]{1,0:T(8,128)(2,1)S(1)}, bf16[96,8192]{1,0:T(8,128)(2,1)S(1)}, u32[]{:S(2)}, u32[]{:S(2)}) collective-permute-start(bf16[96,8192]{1,0:T(8,128)(2,1)S(1)} %constant_dynamic-update-slice_fusion.4.lhs_ref), channel_id=1, source_target_pairs={{0,2},{2,0},{4,6},{6,4},{8,10},{10,8},{12,14},{14,12},{1,3},{3,1},... | collective-permute-start | bytes 4718600 | tf_op jit(solution)/shard_map/ppermute | solution.py:23
  33.7 14.6 %collective-permute-start.1 = (bf16[24,8192]{1,0:T(8,128)(2,1)S(1)}, bf16[24,8192]{1,0:T(8,128)(2,1)S(1)}, u32[]{:S(2)}, u32[]{:S(2)}) collective-permute-start(bf16[24,8192]{1,0:T(8,128)(2,1)S(1)} %collective-permute-done), channel_id=1, source_target_pairs={{0,4},{2,6},{4,8},{6,10},{8,12},{10,14},{12,0},{14,2},{1,5},{3,7},... | collective-permute-start | bytes 1179656 | tf_op jit(solution)/shard_map/ppermute | solution.py:18
  38.0 19.6 %collective-permute-start.2 = (bf16[24,8192]{1,0:T(8,128)(2,1)S(1)}, bf16[24,8192]{1,0:T(8,128)(2,1)S(1)}, u32[]{:S(2)}, u32[]{:S(2)}) collective-permute-start(bf16[24,8192]{1,0:T(8,128)(2,1)S(1)} %collective-permute-done), channel_id=1, source_target_pairs={{0,8},{2,10},{4,12},{6,14},{8,0},{10,2},{12,4},{14,6},{1,9},{3,11}... | collective-permute-start | bytes 1179656 | tf_op jit(solution)/shard_map/ppermute | solution.py:18
  41.6 17.7 %collective-permute-start.3 = (bf16[24,8192]{1,0:T(8,128)(2,1)S(1)}, bf16[24,8192]{1,0:T(8,128)(2,1)S(1)}, u32[]{:S(2)}, u32[]{:S(2)}) collective-permute-start(bf16[24,8192]{1,0:T(8,128)(2,1)S(1)} %collective-permute-done), channel_id=1, source_target_pairs={{0,12},{2,14},{4,0},{6,2},{8,4},{10,6},{12,8},{14,10},{1,13},{3,15... | collective-permute-start | bytes 1179656 | tf_op jit(solution)/shard_map/ppermute | solution.py:18
  59.3 13.7 %collective-permute-start.4 = (bf16[96,8192]{1,0:T(8,128)(2,1)S(1)}, bf16[96,8192]{1,0:T(8,128)(2,1)S(1)}, u32[]{:S(2)}, u32[]{:S(2)}) collective-permute-start(bf16[96,8192]{1,0:T(8,128)(2,1)S(1)} %constant_dynamic-update-slice_fusion.lhs_ref), channel_id=1, source_target_pairs={{0,2},{2,0},{4,6},{6,4},{8,10},{10,8},{12,14},{14,12},{1,3},{3,1},... | collective-permute-start | bytes 4718600 | tf_op jit(solution)/shard_map/ppermute | solution.py:23
  61.3 3.4 %copy-start = (bf16[8192,512]{1,0:T(8,128)(2,1)S(1)}, bf16[8192,512]{1,0:T(8,128)(2,1)}, u32[]{:S(2)}) copy-start(bf16[8192,512]{1,0:T(8,128)(2,1)} %w_ref.7) | copy-start | bytes 25165828
  64.6 3.4 %copy-start.1 = (bf16[8192,512]{1,0:T(8,128)(2,1)S(1)}, bf16[8192,512]{1,0:T(8,128)(2,1)}, u32[]{:S(2)}) copy-start(bf16[8192,512]{1,0:T(8,128)(2,1)} %w_ref.7) | copy-start | bytes 25165828
  73.0 8.2 %copy-start.5 = (s32[24,1]{0,1:T(1,128)S(1)}, s32[24,1]{0,1:T(1,128)}, u32[]{:S(2)}) copy-start(s32[24,1]{0,1:T(1,128)} %param.9) | copy-start | bytes 292
  76.2 20.0 %all-to-all-start.1 = ((bf16[16,24,512]{2,1,0:T(8,128)(2,1)}), bf16[16,24,512]{2,1,0:T(8,128)(2,1)S(1)}, u32[]{:S(2)}, u32[]{:S(2)}) async-start(bf16[16,24,512]{2,1,0:T(8,128)(2,1)} %project.7), calls=%async_computation.1 | async-start | bytes 786432 | tf_op jit(solution)/shard_map/all_to_all | solution.py:208
  96.3 30.5 %all-to-all-start = ((s32[48,1,128]{2,1,0:T(1,128)}), s32[48,1,128]{2,1,0:T(1,128)S(1)}, u32[]{:S(2)}, u32[]{:S(2)}) async-start(s32[48,1,128]{2,1,0:T(1,128)} %count.1), calls=%async_computation | async-start | bytes 49152 | tf_op jit(solution)/shard_map/all_to_all | solution.py:194
  117.0 15.4 %copy-start.3 = (bf16[8192]{0:T(1024)(128)(2,1)S(1)}, bf16[8192]{0:T(1024)(128)(2,1)}, u32[]{:S(2)}) copy-start(bf16[8192]{0:T(1024)(128)(2,1)} %param.11) | copy-start | bytes 49156
  117.0 73.3 %copy-start.2 = (bf16[96,8192]{1,0:T(8,128)(2,1)S(1)}, bf16[96,8192]{1,0:T(8,128)(2,1)}, u32[]{:S(2)}) copy-start(bf16[96,8192]{1,0:T(8,128)(2,1)} %text_ref.1) | copy-start | bytes 4718596
  126.7 63.6 %all-to-all-start.2 = ((bf16[48,2,8192]{2,1,0:T(2,128)(2,1)}), bf16[48,2,8192]{2,1,0:T(2,128)(2,1)S(1)}, u32[]{:S(2)}, u32[]{:S(2)}) async-start(bf16[48,2,8192]{2,1,0:T(2,128)(2,1)} %pack.1), calls=%async_computation.2 | async-start | bytes 3145728 | tf_op jit(solution)/shard_map/all_to_all | solution.py:210

commit v3 on v1

--- a/solution.py
+++ b/solution.py
@@ -69,16 +69,36 @@
     )(*operands)
 
 
-def pack_kernel(route_ref, tokens_ref, out_ref):
+def prepare_kernel(route_ref, gain_ref, slot_ref, wide_ref):
+    rows = route_ref.shape[1]
+    first = lax.broadcasted_iota(jnp.int32, (rows, rows), 0)
+    second = lax.broadcasted_iota(jnp.int32, (rows, rows), 1)
+    across = route_ref[...].astype(jnp.float32)
+    down = jnp.sum(jnp.where(first == second, across, 0.0), axis=1, keepdims=True)
+    earlier = jnp.where((first < second) & (down == across), 1.0, 0.0)
+    slot_ref[...] = 2.0 * across + jnp.sum(earlier, axis=0, keepdims=True)
+    wide_ref[...] = gain_ref[...].astype(jnp.float32)
+
+
+def prepare(route, gain):
+    return pl.pallas_call(
+        prepare_kernel,
+        in_specs=[pl.BlockSpec(memory_space=pltpu.VMEM)] * 2,
+        out_specs=[pl.BlockSpec(memory_space=pltpu.VMEM)] * 2,
+        out_shape=[
+            jax.ShapeDtypeStruct(route.shape, jnp.float32),
+            jax.ShapeDtypeStruct(gain.shape, jnp.float32),
+        ],
+        compiler_params=pltpu.CompilerParams(vmem_limit_bytes=GRANT),
+        name="prepare",
+    )(route, gain)
+
+
+def pack_kernel(slot_ref, tokens_ref, out_ref):
     blocks, rows, width = tokens_ref.shape
     replicas, capacity, _ = out_ref.shape
     slots = replicas * capacity
-    first = lax.broadcasted_iota(jnp.int32, (rows, rows), 0)
-    second = lax.broadcasted_iota(jnp.int32, (rows, rows), 1)
-    down = route_ref[...].astype(jnp.float32)
-    across = jnp.sum(jnp.where(first == second, down, 0.0), axis=0, keepdims=True)
-    earlier = jnp.where((first < second) & (down == across), 1.0, 0.0)
-    slot = 2.0 * across + jnp.sum(earlier, axis=0, keepdims=True)
+    slot = slot_ref[...]
     ids = lax.broadcasted_iota(jnp.int32, (slots, rows), 0).astype(jnp.float32)
     pick = jnp.where(ids == slot, 1.0, 0.0)
     mark = jnp.where(jnp.sum(pick, axis=1, keepdims=True) > 0.0, 0.0, EMPTY)
@@ -89,7 +109,7 @@
         out_ref[:, :, k * width : (k + 1) * width] = moved.reshape(replicas, capacity, width)
 
 
-def pack(route, tokens, replicas, capacity):
+def pack(slot, tokens, replicas, capacity):
     blocks, rows, width = tokens.shape
     slots = replicas * capacity
     return pl.pallas_call(
@@ -104,7 +124,7 @@
         ),
         compiler_params=pltpu.CompilerParams(vmem_limit_bytes=GRANT),
         name="pack",
-    )(route, tokens)
+    )(slot, tokens)
 
 
 def finish_kernel(inbox_ref, text_ref, gain_ref, out_ref, merged):
@@ -132,8 +152,7 @@
     scale_inv = lax.rsqrt(square * (1.0 / width) + 1e-05)
     for k in range(width // step):
         at = slice(k * step, (k + 1) * step)
-        gain = gain_ref[:, at].astype(jnp.float32)
-        out_ref[:, at] = (merged[:, at] * scale_inv * gain).astype(out_ref.dtype)
+        out_ref[:, at] = (merged[:, at] * scale_inv * gain_ref[:, at]).astype(out_ref.dtype)
 
 
 def finish(inbox, text, gain):
@@ -160,6 +179,8 @@
     bias = proj_bias[None, :]
     partner = lax.ppermute(hidden, "tensor", [(0, 1), (1, 0)])
 
+    slot, gain = prepare(route.reshape(1, -1), norm_gain[None, :])
+
     def along_x(block):
         pieces = [block]
         for by in (1, 2, -1):
@@ -173,11 +194,11 @@
         theirs = swap_core(mine)
         blocks = project(theirs, proj_weight, bias, name == "other", True, blocks)
     own = lax.all_to_all(blocks, ("section", "tensor"), split_axis=0, concat_axis=0, tiled=True)
-    outbox = pack(route, own, replicas, capacity)
+    outbox = pack(slot, own, replicas, capacity)
     inbox = lax.all_to_all(
         outbox, "dp", split_axis=0, concat_axis=0, tiled=True
     )
-    return finish(inbox, text, norm_gain[None, :])
+    return finish(inbox, text, gain)
 
 
 def solution(mesh):

time: 180 us -> 178 us (0.989)
  blocking collectives: 0 us -> 77.9 us
  waiting for transfers between devices: 100 us -> 41.4 us
  starting transfers between devices: 57.5 us -> 38.4 us
    all_to_all x0 -> x1, blocking collectives: none -> 77.9 us  [per_device(): lax.all_to_all(outbox, 'dp', split_axis=0, concat_axis=0, tiled=True)]
    all_to_all x1 -> x0, waiting for transfers between devices: 59 us -> none  [per_device(): lax.all_to_all(outbox, 'dp', split_axis=0, concat_axis=0, tiled=True)]
    all_to_all x1 -> x0, starting transfers between devices: 19.1 us -> none  [per_device(): lax.all_to_all(outbox, 'dp', split_axis=0, concat_axis=0, tiled=True)]
    unnamed x19 -> x18, local copies, waits for them, and re-layouts: 5.47 us -> 5.39 us
  transfers between devices with their start and end apart: 11 -> 10, of which waited for: 8 -> 7; matrix products, arithmetic and copies ran while one was open for 1% -> 1% of each run, Pallas kernels for 4% -> 4%
where the time goes in v3:
time: 178 us
  blocking collectives  77.9 us (44%)
  waiting for transfers between devices  41.4 us (23%)
  starting transfers between devices  38.4 us (22%)
  Pallas kernels  14.1 us (8%)
  local copies, waits for them, and re-layouts  5.46 us (3%)
    all_to_all x1, blocking collectives, per_device(): lax.all_to_all(outbox, 'dp', split_axis=0, concat_axis=0, tiled=True)  77.9 us
    ppermute x6, waiting for transfers between devices, shift_x(): return lax.ppermute(block, 'section', pairs)  26.5 us
    ppermute x6, starting transfers between devices, shift_x(): return lax.ppermute(block, 'section', pairs)  22.8 us
    all_to_all x1, waiting for transfers between devices, per_device(): lax.all_to_all(blocks, ('section', 'tensor'), split_axis=0, concat_axis=0...  14.9 us
    pallas_call x4, Pallas kernels, project(): pl.pallas_call(functools.partial(project_kernel, partner, swapped), in_sp...  10.7 us
    ppermute x1, starting transfers between devices, per_device(): partner = lax.ppermute(hidden, 'tensor', [(0, 1), (1, 0)])  6.82 us
    unnamed x18, local copies, waits for them, and re-layouts  5.39 us
    all_to_all x1, starting transfers between devices, per_device(): lax.all_to_all(blocks, ('section', 'tensor'), split_axis=0, concat_axis=0...  4.95 us
  transfers between devices with their start and end apart: 10, of which 7 were waited for; matrix products, arithmetic and copies ran while one was open for 1% of the time, Pallas kernels for 4%

profile of v3, /device:TPU:8, one launch (start us, length us, event | category | flops | bytes accessed | tf_op | source)
XLA Modules:
  0.0 177.5 jit_solution(48812957603450069)
XLA Ops:
  0.0 6.8 %collective-permute-start = (bf16[24,8192]{1,0:T(8,128)(2,1)}, bf16[24,8192]{1,0:T(8,128)(2,1)S(1)}, u32[]{:S(2)}, u32[]{:S(2)}) collective-permute-start(bf16[24,8192]{1,0:T(8,128)(2,1)} %param.6), channel_id=1, source_target_pairs={{0,1},{1,0},{2,3},{3,2},{4,5},{5,4},{6,7},{7,6},{8,9},{9,8},{10,11... | collective-permute-start | bytes 1179656 | tf_op jit(solution)/shard_map/ppermute | solution.py:180
  6.8 3.4 %collective-permute-start.5 = (bf16[24,8192]{1,0:T(8,128)(2,1)}, bf16[24,8192]{1,0:T(8,128)(2,1)S(1)}, u32[]{:S(2)}, u32[]{:S(2)}) collective-permute-start(bf16[24,8192]{1,0:T(8,128)(2,1)} %param.6), channel_id=1, source_target_pairs={{0,4},{2,6},{4,8},{6,10},{8,12},{10,14},{12,0},{14,2},{1,5},{3,7},... | collective-permute-start | bytes 1179656 | tf_op jit(solution)/shard_map/ppermute | solution.py:19
  10.2 4.6 %collective-permute-start.6 = (bf16[24,8192]{1,0:T(8,128)(2,1)}, bf16[24,8192]{1,0:T(8,128)(2,1)S(1)}, u32[]{:S(2)}, u32[]{:S(2)}) collective-permute-start(bf16[24,8192]{1,0:T(8,128)(2,1)} %param.6), channel_id=1, source_target_pairs={{0,8},{2,10},{4,12},{6,14},{8,0},{10,2},{12,4},{14,6},{1,9},{3,11}... | collective-permute-start | bytes 1179656 | tf_op jit(solution)/shard_map/ppermute | solution.py:19
  14.9 3.3 %collective-permute-start.7 = (bf16[24,8192]{1,0:T(8,128)(2,1)}, bf16[24,8192]{1,0:T(8,128)(2,1)S(1)}, u32[]{:S(2)}, u32[]{:S(2)}) collective-permute-start(bf16[24,8192]{1,0:T(8,128)(2,1)} %param.6), channel_id=1, source_target_pairs={{0,12},{2,14},{4,0},{6,2},{8,4},{10,6},{12,8},{14,10},{1,13},{3,15... | collective-permute-start | bytes 1179656 | tf_op jit(solution)/shard_map/ppermute | solution.py:19
  18.2 1.0 constant_dynamic-update-slice_fusion.7
  19.3 1.9 %collective-permute-done.5 = bf16[24,8192]{1,0:T(8,128)(2,1)S(1)} collective-permute-done((bf16[24,8192]{1,0:T(8,128)(2,1)}, bf16[24,8192]{1,0:T(8,128)(2,1)S(1)}, u32[]{:S(2)}, u32[]{:S(2)}) %collective-permute-start.5) | collective-permute-done | bytes 393248 | tf_op jit(solution)/shard_map/ppermute | solution.py:19
  21.2 9.0 %collective-permute-done.6 = bf16[24,8192]{1,0:T(8,128)(2,1)S(1)} collective-permute-done((bf16[24,8192]{1,0:T(8,128)(2,1)}, bf16[24,8192]{1,0:T(8,128)(2,1)S(1)}, u32[]{:S(2)}, u32[]{:S(2)}) %collective-permute-start.6) | collective-permute-done | bytes 393248 | tf_op jit(solution)/shard_map/ppermute | solution.py:19
  30.2 1.5 collective-permute-done.7
  31.7 0.0 copy-start.5
  31.7 1.9 %collective-permute-start.8 = (bf16[96,8192]{1,0:T(8,128)(2,1)S(1)}, bf16[96,8192]{1,0:T(8,128)(2,1)S(1)}, u32[]{:S(2)}, u32[]{:S(2)}) collective-permute-start(bf16[96,8192]{1,0:T(8,128)(2,1)S(1)} %constant_dynamic-update-slice_fusion.4.lhs_ref), channel_id=1, source_target_pairs={{0,2},{2,0},{4,6},{6,4},{8,10},{10,8},{12,14},{14,12},{1,3},{3,1},... | collective-permute-start | bytes 4718600 | tf_op jit(solution)/shard_map/ppermute | solution.py:24
  33.7 0.0 collective-permute-done
  33.7 4.3 %collective-permute-start.1 = (bf16[24,8192]{1,0:T(8,128)(2,1)S(1)}, bf16[24,8192]{1,0:T(8,128)(2,1)S(1)}, u32[]{:S(2)}, u32[]{:S(2)}) collective-permute-start(bf16[24,8192]{1,0:T(8,128)(2,1)S(1)} %collective-permute-done), channel_id=1, source_target_pairs={{0,4},{2,6},{4,8},{6,10},{8,12},{10,14},{12,0},{14,2},{1,5},{3,7},... | collective-permute-start | bytes 1179656 | tf_op jit(solution)/shard_map/ppermute | solution.py:19
  38.0 3.6 %collective-permute-start.2 = (bf16[24,8192]{1,0:T(8,128)(2,1)S(1)}, bf16[24,8192]{1,0:T(8,128)(2,1)S(1)}, u32[]{:S(2)}, u32[]{:S(2)}) collective-permute-start(bf16[24,8192]{1,0:T(8,128)(2,1)S(1)} %collective-permute-done), channel_id=1, source_target_pairs={{0,8},{2,10},{4,12},{6,14},{8,0},{10,2},{12,4},{14,6},{1,9},{3,11}... | collective-permute-start | bytes 1179656 | tf_op jit(solution)/shard_map/ppermute | solution.py:19
  41.6 3.5 %collective-permute-start.3 = (bf16[24,8192]{1,0:T(8,128)(2,1)S(1)}, bf16[24,8192]{1,0:T(8,128)(2,1)S(1)}, u32[]{:S(2)}, u32[]{:S(2)}) collective-permute-start(bf16[24,8192]{1,0:T(8,128)(2,1)S(1)} %collective-permute-done), channel_id=1, source_target_pairs={{0,12},{2,14},{4,0},{6,2},{8,4},{10,6},{12,8},{14,10},{1,13},{3,15... | collective-permute-start | bytes 1179656 | tf_op jit(solution)/shard_map/ppermute | solution.py:19
  45.1 3.2 %collective-permute-done.1 = bf16[24,8192]{1,0:T(8,128)(2,1)S(1)} collective-permute-done((bf16[24,8192]{1,0:T(8,128)(2,1)S(1)}, bf16[24,8192]{1,0:T(8,128)(2,1)S(1)}, u32[]{:S(2)}, u32[]{:S(2)}) %collective-permute-start.1) | collective-permute-done | bytes 393248 | tf_op jit(solution)/shard_map/ppermute | solution.py:19
  48.3 9.3 %collective-permute-done.2 = bf16[24,8192]{1,0:T(8,128)(2,1)S(1)} collective-permute-done((bf16[24,8192]{1,0:T(8,128)(2,1)S(1)}, bf16[24,8192]{1,0:T(8,128)(2,1)S(1)}, u32[]{:S(2)}, u32[]{:S(2)}) %collective-permute-start.2) | collective-permute-done | bytes 393248 | tf_op jit(solution)/shard_map/ppermute | solution.py:19
  57.6 1.7 collective-permute-done.3
  59.3 1.9 %collective-permute-start.4 = (bf16[96,8192]{1,0:T(8,128)(2,1)S(1)}, bf16[96,8192]{1,0:T(8,128)(2,1)S(1)}, u32[]{:S(2)}, u32[]{:S(2)}) collective-permute-start(bf16[96,8192]{1,0:T(8,128)(2,1)S(1)} %constant_dynamic-update-slice_fusion.lhs_ref), channel_id=1, source_target_pairs={{0,2},{2,0},{4,6},{6,4},{8,10},{10,8},{12,14},{14,12},{1,3},{3,1},... | collective-permute-start | bytes 4718600 | tf_op jit(solution)/shard_map/ppermute | solution.py:24
  61.2 0.0 copy-done.5
  61.3 0.0 copy-start
  61.3 3.4 %copy-done = bf16[8192,512]{1,0:T(8,128)(2,1)S(1)} copy-done((bf16[8192,512]{1,0:T(8,128)(2,1)S(1)}, bf16[8192,512]{1,0:T(8,128)(2,1)}, u32[]{:S(2)}) %copy-start) | copy-done | bytes 8388632
  64.6 0.0 copy-start.1
  64.7 2.5 %project.4.rest_0_ = bf16[16,24,512]{2,1,0:T(8,128)(2,1)S(1)} custom-call(bf16[96,8192]{1,0:T(8,128)(2,1)S(1)} %constant_dynamic-update-slice_fusion.4.lhs_ref, bf16[8192,512]{1,0:T(8,128)(2,1)S(1)} %copy-done, bf16[1,512]{1,0:T(2,128)(2,1)S(1)} %broadcast_in_dim.7.bias_ref), custom_call_target="tpu_custom_call" | custom-call | flops 805306368 | bytes 10059776 | tf_op jit(solution)/shard_map/project/pallas_call | solution.py:56
  67.2 0.0 collective-permute-done.8.lhs_ref
  67.2 0.8 copy-done.1
  68.0 2.5 %project.5.rest_0_ = bf16[16,24,512]{2,1,0:T(8,128)(2,1)S(1)} custom-call(bf16[96,8192]{1,0:T(8,128)(2,1)S(1)} %collective-permute-done.8.lhs_ref, bf16[8192,512]{1,0:T(8,128)(2,1)S(1)} %copy-done.1, bf16[1,512]{1,0:T(2,128)(2,1)S(1)} %broadcast_in_dim.7.bias_ref, bf16[16,24,512]{2,1,0:T(8,128)(2,1)S(1)} %project.4.rest_0_), custom_call_target="tpu_custom_call" | custom-call | flops 805306368 | bytes 10059776 | tf_op jit(solution)/shard_map/project/pallas_call | solution.py:56
  70.5 2.5 %project.6.rest_0_ = bf16[16,24,512]{2,1,0:T(8,128)(2,1)S(1)} custom-call(bf16[96,8192]{1,0:T(8,128)(2,1)S(1)} %constant_dynamic-update-slice_fusion.lhs_ref, bf16[8192,512]{1,0:T(8,128)(2,1)S(1)} %copy-done.1, bf16[1,512]{1,0:T(2,128)(2,1)S(1)} %broadcast_in_dim.7.bias_ref, bf16[16,24,512]{2,1,0:T(8,128)(2,1)S(1)} %project.5.rest_0_), custom_call_target="tpu_custom_call" | custom-call | flops 805306368 | bytes 10059776 | tf_op jit(solution)/shard_map/project/pallas_call | solution.py:56
  73.0 0.0 copy-start.4
  73.0 0.0 copy-start.3
  73.0 0.0 collective-permute-done.4.lhs_ref
  73.0 3.2 %project.7 = bf16[16,24,512]{2,1,0:T(8,128)(2,1)} custom-call(bf16[96,8192]{1,0:T(8,128)(2,1)S(1)} %collective-permute-done.4.lhs_ref, bf16[8192,512]{1,0:T(8,128)(2,1)S(1)} %copy-done.1, bf16[1,512]{1,0:T(2,128)(2,1)S(1)} %broadcast_in_dim.7.bias_ref, bf16[16,24,512]{2,1,0:T(8,128)(2,1)S(1)} %project.6.rest_0_), custom_call_target="tpu_custom_call" | custom-call | flops 805306368 | bytes 10059776 | tf_op jit(solution)/shard_map/project/pallas_call | solution.py:56
  76.3 4.9 %all-to-all-start = ((bf16[16,24,512]{2,1,0:T(8,128)(2,1)}), bf16[16,24,512]{2,1,0:T(8,128)(2,1)S(1)}, u32[]{:S(2)}, u32[]{:S(2)}) async-start(bf16[16,24,512]{2,1,0:T(8,128)(2,1)} %project.7), calls=%async_computation | async-start | bytes 786432 | tf_op jit(solution)/shard_map/all_to_all | solution.py:196
  81.2 0.0 copy-done.4
  81.2 0.0 copy-done.3
  81.3 0.1 prepare.1
  81.4 14.9 %all-to-all-done.tokens_ref = bf16[16,24,512]{2,1,0:T(8,128)(2,1)S(1)} async-done(((bf16[16,24,512]{2,1,0:T(8,128)(2,1)}), bf16[16,24,512]{2,1,0:T(8,128)(2,1)S(1)}, u32[]{:S(2)}, u32[]{:S(2)}) %all-to-all-start) | async-done | bytes 393248 | tf_op jit(solution)/shard_map/all_to_all | solution.py:196
  96.3 0.6 pack.1
  96.9 0.0 copy-start.2
  96.9 77.9 %all_to_all.10.inbox_ref = bf16[48,2,8192]{2,1,0:T(2,128)(2,1)S(1)} all-to-all(bf16[48,2,8192]{2,1,0:T(2,128)(2,1)S(1)} %pack.1), channel_id=1, replica_groups=mesh['dp'=48,'section'=8,'tensor'=2] {'dp'}, dimensions={0} | all-to-all | bytes 3145728 | tf_op jit(solution)/shard_map/all_to_all | solution.py:198
  174.8 0.0 copy-done.2
  174.8 2.7 %finish.1 = bf16[96,8192]{1,0:T(8,128)(2,1)} custom-call(bf16[48,2,8192]{2,1,0:T(2,128)(2,1)S(1)} %all_to_all.10.inbox_ref, bf16[96,8192]{1,0:T(8,128)(2,1)S(1)} %copy-done.2, f32[1,8192]{1,0:T(1,128)S(1)} %get-tuple-element.8.gain_ref), custom_call_target="tpu_custom_call" | custom-call | flops 150994944 | bytes 4718592 | tf_op jit(solution)/shard_map/finish/pallas_call | solution.py:160
  (9 shorter events, 0.2 us)
Async XLA Ops:
  0.0 33.7 %collective-permute-start = (bf16[24,8192]{1,0:T(8,128)(2,1)}, bf16[24,8192]{1,0:T(8,128)(2,1)S(1)}, u32[]{:S(2)}, u32[]{:S(2)}) collective-permute-start(bf16[24,8192]{1,0:T(8,128)(2,1)} %param.6), channel_id=1, source_target_pairs={{0,1},{1,0},{2,3},{3,2},{4,5},{5,4},{6,7},{7,6},{8,9},{9,8},{10,11... | collective-permute-start | bytes 1179656 | tf_op jit(solution)/shard_map/ppermute | solution.py:180
  6.8 14.3 %collective-permute-start.5 = (bf16[24,8192]{1,0:T(8,128)(2,1)}, bf16[24,8192]{1,0:T(8,128)(2,1)S(1)}, u32[]{:S(2)}, u32[]{:S(2)}) collective-permute-start(bf16[24,8192]{1,0:T(8,128)(2,1)} %param.6), channel_id=1, source_target_pairs={{0,4},{2,6},{4,8},{6,10},{8,12},{10,14},{12,0},{14,2},{1,5},{3,7},... | collective-permute-start | bytes 1179656 | tf_op jit(solution)/shard_map/ppermute | solution.py:19
  10.2 19.9 %collective-permute-start.6 = (bf16[24,8192]{1,0:T(8,128)(2,1)}, bf16[24,8192]{1,0:T(8,128)(2,1)S(1)}, u32[]{:S(2)}, u32[]{:S(2)}) collective-permute-start(bf16[24,8192]{1,0:T(8,128)(2,1)} %param.6), channel_id=1, source_target_pairs={{0,8},{2,10},{4,12},{6,14},{8,0},{10,2},{12,4},{14,6},{1,9},{3,11}... | collective-permute-start | bytes 1179656 | tf_op jit(solution)/shard_map/ppermute | solution.py:19
  14.9 16.8 %collective-permute-start.7 = (bf16[24,8192]{1,0:T(8,128)(2,1)}, bf16[24,8192]{1,0:T(8,128)(2,1)S(1)}, u32[]{:S(2)}, u32[]{:S(2)}) collective-permute-start(bf16[24,8192]{1,0:T(8,128)(2,1)} %param.6), channel_id=1, source_target_pairs={{0,12},{2,14},{4,0},{6,2},{8,4},{10,6},{12,8},{14,10},{1,13},{3,15... | collective-permute-start | bytes 1179656 | tf_op jit(solution)/shard_map/ppermute | solution.py:19
  31.7 29.5 %copy-start.5 = (bf16[512]{0:T(512)(128)(2,1)S(1)}, bf16[512]{0:T(512)(128)(2,1)}, u32[]{:S(2)}) copy-start(bf16[512]{0:T(512)(128)(2,1)} %param.8) | copy-start | bytes 3076
  31.7 35.5 %collective-permute-start.8 = (bf16[96,8192]{1,0:T(8,128)(2,1)S(1)}, bf16[96,8192]{1,0:T(8,128)(2,1)S(1)}, u32[]{:S(2)}, u32[]{:S(2)}) collective-permute-start(bf16[96,8192]{1,0:T(8,128)(2,1)S(1)} %constant_dynamic-update-slice_fusion.4.lhs_ref), channel_id=1, source_target_pairs={{0,2},{2,0},{4,6},{6,4},{8,10},{10,8},{12,14},{14,12},{1,3},{3,1},... | collective-permute-start | bytes 4718600 | tf_op jit(solution)/shard_map/ppermute | solution.py:24
  33.7 14.6 %collective-permute-start.1 = (bf16[24,8192]{1,0:T(8,128)(2,1)S(1)}, bf16[24,8192]{1,0:T(8,128)(2,1)S(1)}, u32[]{:S(2)}, u32[]{:S(2)}) collective-permute-start(bf16[24,8192]{1,0:T(8,128)(2,1)S(1)} %collective-permute-done), channel_id=1, source_target_pairs={{0,4},{2,6},{4,8},{6,10},{8,12},{10,14},{12,0},{14,2},{1,5},{3,7},... | collective-permute-start | bytes 1179656 | tf_op jit(solution)/shard_map/ppermute | solution.py:19
  38.0 19.6 %collective-permute-start.2 = (bf16[24,8192]{1,0:T(8,128)(2,1)S(1)}, bf16[24,8192]{1,0:T(8,128)(2,1)S(1)}, u32[]{:S(2)}, u32[]{:S(2)}) collective-permute-start(bf16[24,8192]{1,0:T(8,128)(2,1)S(1)} %collective-permute-done), channel_id=1, source_target_pairs={{0,8},{2,10},{4,12},{6,14},{8,0},{10,2},{12,4},{14,6},{1,9},{3,11}... | collective-permute-start | bytes 1179656 | tf_op jit(solution)/shard_map/ppermute | solution.py:19
  41.6 17.7 %collective-permute-start.3 = (bf16[24,8192]{1,0:T(8,128)(2,1)S(1)}, bf16[24,8192]{1,0:T(8,128)(2,1)S(1)}, u32[]{:S(2)}, u32[]{:S(2)}) collective-permute-start(bf16[24,8192]{1,0:T(8,128)(2,1)S(1)} %collective-permute-done), channel_id=1, source_target_pairs={{0,12},{2,14},{4,0},{6,2},{8,4},{10,6},{12,8},{14,10},{1,13},{3,15... | collective-permute-start | bytes 1179656 | tf_op jit(solution)/shard_map/ppermute | solution.py:19
  59.3 13.7 %collective-permute-start.4 = (bf16[96,8192]{1,0:T(8,128)(2,1)S(1)}, bf16[96,8192]{1,0:T(8,128)(2,1)S(1)}, u32[]{:S(2)}, u32[]{:S(2)}) collective-permute-start(bf16[96,8192]{1,0:T(8,128)(2,1)S(1)} %constant_dynamic-update-slice_fusion.lhs_ref), channel_id=1, source_target_pairs={{0,2},{2,0},{4,6},{6,4},{8,10},{10,8},{12,14},{14,12},{1,3},{3,1},... | collective-permute-start | bytes 4718600 | tf_op jit(solution)/shard_map/ppermute | solution.py:24
  61.3 3.4 %copy-start = (bf16[8192,512]{1,0:T(8,128)(2,1)S(1)}, bf16[8192,512]{1,0:T(8,128)(2,1)}, u32[]{:S(2)}) copy-start(bf16[8192,512]{1,0:T(8,128)(2,1)} %w_ref.7) | copy-start | bytes 25165828
  64.6 3.4 %copy-start.1 = (bf16[8192,512]{1,0:T(8,128)(2,1)S(1)}, bf16[8192,512]{1,0:T(8,128)(2,1)}, u32[]{:S(2)}) copy-start(bf16[8192,512]{1,0:T(8,128)(2,1)} %w_ref.7) | copy-start | bytes 25165828
  73.0 8.2 %copy-start.4 = (bf16[8192]{0:T(1024)(128)(2,1)S(1)}, bf16[8192]{0:T(1024)(128)(2,1)}, u32[]{:S(2)}) copy-start(bf16[8192]{0:T(1024)(128)(2,1)} %param.11) | copy-start | bytes 49156
  73.0 8.2 %copy-start.3 = (s32[24,1]{0,1:T(1,128)S(1)}, s32[24,1]{0,1:T(1,128)}, u32[]{:S(2)}) copy-start(s32[24,1]{0,1:T(1,128)} %param.9) | copy-start | bytes 292
  76.3 20.0 %all-to-all-start = ((bf16[16,24,512]{2,1,0:T(8,128)(2,1)}), bf16[16,24,512]{2,1,0:T(8,128)(2,1)S(1)}, u32[]{:S(2)}, u32[]{:S(2)}) async-start(bf16[16,24,512]{2,1,0:T(8,128)(2,1)} %project.7), calls=%async_computation | async-start | bytes 786432 | tf_op jit(solution)/shard_map/all_to_all | solution.py:196
  96.9 77.9 %copy-start.2 = (bf16[96,8192]{1,0:T(8,128)(2,1)S(1)}, bf16[96,8192]{1,0:T(8,128)(2,1)}, u32[]{:S(2)}) copy-start(bf16[96,8192]{1,0:T(8,128)(2,1)} %text_ref.1) | copy-start | bytes 4718596

commit v4 on v3

--- a/solution.py
+++ b/solution.py
@@ -38,14 +38,13 @@
     if len(rest) == 3:
         out_ref[...] = rest[0][...]
     section = lax.axis_index("section")
-    tensor = lax.axis_index("tensor")
     x, core = section // 2, section % 2
-    t = (1 - tensor) if partner else tensor
     c = (1 - core) if swapped else core
     rows = out_ref.shape[1]
     bias = bias_ref[...].astype(jnp.float32)
     for k in range(NX):
-        dst = (lax.rem(x - k + NX, NX) * 2 + c) * 2 + t
+        from_x = lax.rem(x - k + NX, NX)
+        dst = from_x if partner else from_x * 2 + c
         out_ref[dst] = (acc[k * rows : (k + 1) * rows, :] + bias).astype(out_ref.dtype)
 
 
@@ -53,11 +52,12 @@
     rows, depth = lhs.shape
     width = weight.shape[1]
     operands = [lhs, weight, bias] + ([] if base is None else [base])
+    blocks = NX if partner else 2 * NX
     return pl.pallas_call(
         functools.partial(project_kernel, partner, swapped),
         in_specs=[pl.BlockSpec(memory_space=pltpu.VMEM)] * len(operands),
         out_specs=pl.BlockSpec(memory_space=pltpu.VMEM),
-        out_shape=jax.ShapeDtypeStruct((4 * NX, rows // NX, width), jnp.bfloat16),
+        out_shape=jax.ShapeDtypeStruct((blocks, rows // NX, width), jnp.bfloat16),
         scratch_shapes=[pltpu.VMEM((rows, width), jnp.float32)],
         compiler_params=pltpu.CompilerParams(vmem_limit_bytes=GRANT),
         cost_estimate=pl.CostEstimate(
@@ -67,6 +67,29 @@
         ),
         name="project",
     )(*operands)
+
+
+def join_kernel(own_ref, same_ref, swapped_ref, out_ref):
+    core = lax.axis_index("section") % 2
+    tensor = lax.axis_index("tensor")
+    width = own_ref.shape[2]
+    out_ref[:, :, pl.ds(pl.multiple_of(tensor * width, width), width)] = own_ref[...]
+    rest = pl.ds(pl.multiple_of((1 - tensor) * width, width), width)
+    for x in range(NX):
+        out_ref[2 * x + core, :, rest] = same_ref[x]
+        out_ref[2 * x + 1 - core, :, rest] = swapped_ref[x]
+
+
+def join(own, same, swapped):
+    blocks, rows, width = own.shape
+    return pl.pallas_call(
+        join_kernel,
+        in_specs=[pl.BlockSpec(memory_space=pltpu.VMEM)] * 3,
+        out_specs=pl.BlockSpec(memory_space=pltpu.VMEM),
+        out_shape=jax.ShapeDtypeStruct((blocks, rows, 2 * width), own.dtype),
+        compiler_params=pltpu.CompilerParams(vmem_limit_bytes=GRANT),
+        name="join",
+    )(own, same, swapped)
 
 
 def prepare_kernel(route_ref, gain_ref, slot_ref, wide_ref):
@@ -187,13 +210,19 @@
             pieces.append(shift_x(block, by))
         return jnp.concatenate(pieces, axis=0)
 
-    blocks = None
-    for name, block in (("own", hidden), ("other", partner)):
-        mine = along_x(block)
-        blocks = project(mine, proj_weight, bias, name == "other", False, blocks)
-        theirs = swap_core(mine)
-        blocks = project(theirs, proj_weight, bias, name == "other", True, blocks)
-    own = lax.all_to_all(blocks, ("section", "tensor"), split_axis=0, concat_axis=0, tiled=True)
+    def send_back(block):
+        return lax.ppermute(block, "tensor", [(0, 1), (1, 0)])
+
+    mine = along_x(hidden)
+    kept = project(mine, proj_weight, bias, False, False)
+    theirs = swap_core(mine)
+    kept = project(theirs, proj_weight, bias, False, True, kept)
+    mine = along_x(partner)
+    same = project(mine, proj_weight, bias, True, False)
+    theirs = swap_core(mine)
+    swapped = project(theirs, proj_weight, bias, True, True)
+    blocks = join(kept, send_back(same), send_back(swapped))
+    own = lax.all_to_all(blocks, "section", split_axis=0, concat_axis=0, tiled=True)
     outbox = pack(slot, own, replicas, capacity)
     inbox = lax.all_to_all(
         outbox, "dp", split_axis=0, concat_axis=0, tiled=True

time: 178 us -> 175 us (0.983)
  the two profiles are of different devices: /device:TPU:8 before, /device:TPU:16 now
where the time goes in v4:
time: 175 us; the launch traced here: 174 us
  blocking collectives  77 us (44%)
  starting transfers between devices  50.5 us (29%)
  waiting for transfers between devices  27.4 us (16%)
  Pallas kernels  14.2 us (8%)
  local copies, waits for them, and re-layouts  4.66 us (3%)
    all_to_all x1, blocking collectives, per_device(): lax.all_to_all(outbox, 'dp', split_axis=0, concat_axis=0, tiled=True)  77 us
    ppermute x6, starting transfers between devices, shift_x(): return lax.ppermute(block, 'section', pairs)  26.3 us
    ppermute x6, waiting for transfers between devices, shift_x(): return lax.ppermute(block, 'section', pairs)  13.2 us
    pallas_call x4, Pallas kernels, project(): pl.pallas_call(functools.partial(project_kernel, partner, swapped), in_sp...  10 us
    ppermute x2, starting transfers between devices, send_back(): return lax.ppermute(block, 'tensor', [(0, 1), (1, 0)])  10 us
    all_to_all x1, waiting for transfers between devices, per_device(): lax.all_to_all(blocks, 'section', split_axis=0, concat_axis=0, tiled=True)  8.77 us
    ppermute x1, starting transfers between devices, per_device(): partner = lax.ppermute(hidden, 'tensor', [(0, 1), (1, 0)])  5.92 us
    unnamed x20, local copies, waits for them, and re-layouts  4.58 us
  transfers between devices with their start and end apart: 12, of which 6 were waited for; matrix products, arithmetic and copies ran while one was open for 1% of the time, Pallas kernels for 6%

profile of v4, /device:TPU:16, one launch (start us, length us, event | category | flops | bytes accessed | tf_op | source)
XLA Modules:
  0.0 174.0 jit_solution(17672050179292134072)
XLA Ops:
  0.0 5.9 %collective-permute-start.4 = (bf16[24,8192]{1,0:T(8,128)(2,1)}, bf16[24,8192]{1,0:T(8,128)(2,1)S(1)}, u32[]{:S(2)}, u32[]{:S(2)}) collective-permute-start(bf16[24,8192]{1,0:T(8,128)(2,1)} %param.6), channel_id=1, source_target_pairs={{0,1},{1,0},{2,3},{3,2},{4,5},{5,4},{6,7},{7,6},{8,9},{9,8},{10,11... | collective-permute-start | bytes 1179656 | tf_op jit(solution)/shard_map/ppermute | solution.py:203
  5.9 3.4 %collective-permute-start = (bf16[24,8192]{1,0:T(8,128)(2,1)}, bf16[24,8192]{1,0:T(8,128)(2,1)S(1)}, u32[]{:S(2)}, u32[]{:S(2)}) collective-permute-start(bf16[24,8192]{1,0:T(8,128)(2,1)} %param.6), channel_id=1, source_target_pairs={{0,4},{2,6},{4,8},{6,10},{8,12},{10,14},{12,0},{14,2},{1,5},{3,7},... | collective-permute-start | bytes 1179656 | tf_op jit(solution)/shard_map/ppermute | solution.py:19
  9.3 4.6 %collective-permute-start.1 = (bf16[24,8192]{1,0:T(8,128)(2,1)}, bf16[24,8192]{1,0:T(8,128)(2,1)S(1)}, u32[]{:S(2)}, u32[]{:S(2)}) collective-permute-start(bf16[24,8192]{1,0:T(8,128)(2,1)} %param.6), channel_id=1, source_target_pairs={{0,8},{2,10},{4,12},{6,14},{8,0},{10,2},{12,4},{14,6},{1,9},{3,11}... | collective-permute-start | bytes 1179656 | tf_op jit(solution)/shard_map/ppermute | solution.py:19
  14.0 3.3 %collective-permute-start.2 = (bf16[24,8192]{1,0:T(8,128)(2,1)}, bf16[24,8192]{1,0:T(8,128)(2,1)S(1)}, u32[]{:S(2)}, u32[]{:S(2)}) collective-permute-start(bf16[24,8192]{1,0:T(8,128)(2,1)} %param.6), channel_id=1, source_target_pairs={{0,12},{2,14},{4,0},{6,2},{8,4},{10,6},{12,8},{14,10},{1,13},{3,15... | collective-permute-start | bytes 1179656 | tf_op jit(solution)/shard_map/ppermute | solution.py:19
  17.3 1.0 constant_dynamic-update-slice_fusion.3
  18.4 3.5 %collective-permute-done.4 = bf16[24,8192]{1,0:T(8,128)(2,1)S(1)} collective-permute-done((bf16[24,8192]{1,0:T(8,128)(2,1)}, bf16[24,8192]{1,0:T(8,128)(2,1)S(1)}, u32[]{:S(2)}, u32[]{:S(2)}) %collective-permute-start.4) | collective-permute-done | bytes 393248 | tf_op jit(solution)/shard_map/ppermute | solution.py:203
  21.9 7.0 %collective-permute-start.5 = (bf16[24,8192]{1,0:T(8,128)(2,1)S(1)}, bf16[24,8192]{1,0:T(8,128)(2,1)S(1)}, u32[]{:S(2)}, u32[]{:S(2)}) collective-permute-start(bf16[24,8192]{1,0:T(8,128)(2,1)S(1)} %collective-permute-done.4), channel_id=1, source_target_pairs={{0,4},{2,6},{4,8},{6,10},{8,12},{10,14},{12,0},{14,2},{1,5},{3,7},... | collective-permute-start | bytes 1179656 | tf_op jit(solution)/shard_map/ppermute | solution.py:19
  28.9 4.6 %collective-permute-start.6 = (bf16[24,8192]{1,0:T(8,128)(2,1)S(1)}, bf16[24,8192]{1,0:T(8,128)(2,1)S(1)}, u32[]{:S(2)}, u32[]{:S(2)}) collective-permute-start(bf16[24,8192]{1,0:T(8,128)(2,1)S(1)} %collective-permute-done.4), channel_id=1, source_target_pairs={{0,8},{2,10},{4,12},{6,14},{8,0},{10,2},{12,4},{14,6},{1,9},{3,11}... | collective-permute-start | bytes 1179656 | tf_op jit(solution)/shard_map/ppermute | solution.py:19
  33.5 0.0 collective-permute-done
  33.5 3.3 %collective-permute-start.7 = (bf16[24,8192]{1,0:T(8,128)(2,1)S(1)}, bf16[24,8192]{1,0:T(8,128)(2,1)S(1)}, u32[]{:S(2)}, u32[]{:S(2)}) collective-permute-start(bf16[24,8192]{1,0:T(8,128)(2,1)S(1)} %collective-permute-done.4), channel_id=1, source_target_pairs={{0,12},{2,14},{4,0},{6,2},{8,4},{10,6},{12,8},{14,10},{1,13},{3,15... | collective-permute-start | bytes 1179656 | tf_op jit(solution)/shard_map/ppermute | solution.py:19
  36.9 0.0 collective-permute-done.1
  37.0 0.0 copy-start.4
  37.0 2.3 %collective-permute-done.5 = bf16[24,8192]{1,0:T(8,128)(2,1)S(1)} collective-permute-done((bf16[24,8192]{1,0:T(8,128)(2,1)S(1)}, bf16[24,8192]{1,0:T(8,128)(2,1)S(1)}, u32[]{:S(2)}, u32[]{:S(2)}) %collective-permute-start.5) | collective-permute-done | bytes 393248 | tf_op jit(solution)/shard_map/ppermute | solution.py:19
  39.3 9.6 %collective-permute-done.6 = bf16[24,8192]{1,0:T(8,128)(2,1)S(1)} collective-permute-done((bf16[24,8192]{1,0:T(8,128)(2,1)S(1)}, bf16[24,8192]{1,0:T(8,128)(2,1)S(1)}, u32[]{:S(2)}, u32[]{:S(2)}) %collective-permute-start.6) | collective-permute-done | bytes 393248 | tf_op jit(solution)/shard_map/ppermute | solution.py:19
  48.9 1.3 collective-permute-done.7
  50.2 1.9 %collective-permute-start.9 = (bf16[96,8192]{1,0:T(8,128)(2,1)S(1)}, bf16[96,8192]{1,0:T(8,128)(2,1)S(1)}, u32[]{:S(2)}, u32[]{:S(2)}) collective-permute-start(bf16[96,8192]{1,0:T(8,128)(2,1)S(1)} %constant_dynamic-update-slice_fusion.4.lhs_ref), channel_id=1, source_target_pairs={{0,2},{2,0},{4,6},{6,4},{8,10},{10,8},{12,14},{14,12},{1,3},{3,1},... | collective-permute-start | bytes 4718600 | tf_op jit(solution)/shard_map/ppermute | solution.py:24
  52.2 0.0 collective-permute-done.2
  52.2 2.4 %collective-permute-start.3 = (bf16[96,8192]{1,0:T(8,128)(2,1)S(1)}, bf16[96,8192]{1,0:T(8,128)(2,1)S(1)}, u32[]{:S(2)}, u32[]{:S(2)}) collective-permute-start(bf16[96,8192]{1,0:T(8,128)(2,1)S(1)} %constant_dynamic-update-slice_fusion.lhs_ref), channel_id=1, source_target_pairs={{0,2},{2,0},{4,6},{6,4},{8,10},{10,8},{12,14},{14,12},{1,3},{3,1},... | collective-permute-start | bytes 4718600 | tf_op jit(solution)/shard_map/ppermute | solution.py:24
  54.6 0.0 copy-done.4
  54.7 0.0 copy-start
  54.7 3.4 %copy-done = bf16[8192,512]{1,0:T(8,128)(2,1)S(1)} copy-done((bf16[8192,512]{1,0:T(8,128)(2,1)S(1)}, bf16[8192,512]{1,0:T(8,128)(2,1)}, u32[]{:S(2)}) %copy-start) | copy-done | bytes 8388632
  58.0 0.0 slice-start
  58.0 2.5 %project.6 = bf16[4,24,512]{2,1,0:T(8,128)(2,1)S(1)} custom-call(bf16[96,8192]{1,0:T(8,128)(2,1)S(1)} %constant_dynamic-update-slice_fusion.4.lhs_ref, bf16[8192,512]{1,0:T(8,128)(2,1)S(1)} %copy-done, bf16[1,512]{1,0:T(2,128)(2,1)S(1)} %broadcast_in_dim.7.bias_ref), custom_call_target="tpu_custom_call" | custom-call | flops 805306368 | bytes 10059776 | tf_op jit(solution)/shard_map/project/pallas_call | solution.py:56
  60.6 0.0 slice-start.1
  60.6 5.0 %collective-permute-start.8 = (bf16[4,24,512]{2,1,0:T(8,128)(2,1)S(1)}, bf16[4,24,512]{2,1,0:T(8,128)(2,1)S(1)}, u32[]{:S(2)}, u32[]{:S(2)}) collective-permute-start(bf16[4,24,512]{2,1,0:T(8,128)(2,1)S(1)} %project.6), channel_id=1, source_target_pairs={{0,1},{1,0},{2,3},{3,2},{4,5},{5,4},{6,7},{7,6},{8,9},{9,8},{10,11... | collective-permute-start | bytes 294920 | tf_op jit(solution)/shard_map/ppermute | solution.py:214
  65.6 0.0 collective-permute-done.9.lhs_ref
  65.7 2.5 %project.7 = bf16[4,24,512]{2,1,0:T(8,128)(2,1)S(1)} custom-call(bf16[96,8192]{1,0:T(8,128)(2,1)S(1)} %collective-permute-done.9.lhs_ref, bf16[8192,512]{1,0:T(8,128)(2,1)S(1)} %copy-done, bf16[1,512]{1,0:T(2,128)(2,1)S(1)} %broadcast_in_dim.7.bias_ref), custom_call_target="tpu_custom_call" | custom-call | flops 805306368 | bytes 10059776 | tf_op jit(solution)/shard_map/project/pallas_call | solution.py:56
  68.2 5.0 %collective-permute-start.10 = (bf16[4,24,512]{2,1,0:T(8,128)(2,1)S(1)}, bf16[4,24,512]{2,1,0:T(8,128)(2,1)S(1)}, u32[]{:S(2)}, u32[]{:S(2)}) collective-permute-start(bf16[4,24,512]{2,1,0:T(8,128)(2,1)S(1)} %project.7), channel_id=1, source_target_pairs={{0,1},{1,0},{2,3},{3,2},{4,5},{5,4},{6,7},{7,6},{8,9},{9,8},{10,11... | collective-permute-start | bytes 294920 | tf_op jit(solution)/shard_map/ppermute | solution.py:214
  73.2 0.0 slice-done
  73.2 0.0 slice-done.1
  73.2 2.5 %project.4.rest_0_ = bf16[8,24,512]{2,1,0:T(8,128)(2,1)S(1)} custom-call(bf16[96,8192]{1,0:T(8,128)(2,1)S(1)} %constant_dynamic-update-slice_fusion.lhs_ref, bf16[8192,512]{1,0:T(8,128)(2,1)S(1)} %bitcast.2, bf16[1,512]{1,0:T(2,128)(2,1)S(1)} %broadcast_in_dim.7.bias_ref), custom_call_target="tpu_custom_call" | custom-call | flops 805306368 | bytes 10059776 | tf_op jit(solution)/shard_map/project/pallas_call | solution.py:56
  75.7 0.0 collective-permute-done.3.lhs_ref
  75.7 2.5 %project.5.own_ref = bf16[8,24,512]{2,1,0:T(8,128)(2,1)S(1)} custom-call(bf16[96,8192]{1,0:T(8,128)(2,1)S(1)} %collective-permute-done.3.lhs_ref, bf16[8192,512]{1,0:T(8,128)(2,1)S(1)} %bitcast.2, bf16[1,512]{1,0:T(2,128)(2,1)S(1)} %broadcast_in_dim.7.bias_ref, bf16[8,24,512]{2,1,0:T(8,128)(2,1)S(1)} %project.4.rest_0_), custom_call_target="tpu_custom_call" | custom-call | flops 805306368 | bytes 10059776 | tf_op jit(solution)/shard_map/project/pallas_call | solution.py:56
  78.2 0.0 copy-start.3
  78.2 0.0 copy-start.2
  78.2 0.0 collective-permute-done.8.same_ref
  78.2 1.9 %collective-permute-done.10.swapped_ref = bf16[4,24,512]{2,1,0:T(8,128)(2,1)S(1)} collective-permute-done((bf16[4,24,512]{2,1,0:T(8,128)(2,1)S(1)}, bf16[4,24,512]{2,1,0:T(8,128)(2,1)S(1)}, u32[]{:S(2)}, u32[]{:S(2)}) %collective-permute-start.10) | collective-permute-done | bytes 98336 | tf_op jit(solution)/shard_map/ppermute | solution.py:214
  80.1 0.8 join.1
  80.9 3.9 %all-to-all-start = ((bf16[8,24,1024]{2,1,0:T(8,128)(2,1)}), bf16[8,24,1024]{2,1,0:T(8,128)(2,1)S(1)}, u32[]{:S(2)}, u32[]{:S(2)}) async-start(bf16[8,24,1024]{2,1,0:T(8,128)(2,1)} %join.1), calls=%async_computation | async-start | bytes 786432 | tf_op jit(solution)/shard_map/all_to_all | solution.py:225
  84.8 0.0 copy-done.3
  84.8 0.0 copy-done.2
  84.8 0.1 prepare.1
  84.9 8.8 %all-to-all-done.tokens_ref = bf16[8,24,1024]{2,1,0:T(8,128)(2,1)S(1)} async-done(((bf16[8,24,1024]{2,1,0:T(8,128)(2,1)}), bf16[8,24,1024]{2,1,0:T(8,128)(2,1)S(1)}, u32[]{:S(2)}, u32[]{:S(2)}) %all-to-all-start) | async-done | bytes 393248 | tf_op jit(solution)/shard_map/all_to_all | solution.py:225
  93.7 0.6 pack.1
  94.3 0.0 copy-start.1
  94.3 77.0 %all_to_all.10.inbox_ref = bf16[48,2,8192]{2,1,0:T(2,128)(2,1)S(1)} all-to-all(bf16[48,2,8192]{2,1,0:T(2,128)(2,1)S(1)} %pack.1), channel_id=1, replica_groups=mesh['dp'=48,'section'=8,'tensor'=2] {'dp'}, dimensions={0} | all-to-all | bytes 3145728 | tf_op jit(solution)/shard_map/all_to_all | solution.py:227
  171.3 0.0 copy-done.1
  171.3 2.7 %finish.1 = bf16[96,8192]{1,0:T(8,128)(2,1)} custom-call(bf16[48,2,8192]{2,1,0:T(2,128)(2,1)S(1)} %all_to_all.10.inbox_ref, bf16[96,8192]{1,0:T(8,128)(2,1)S(1)} %copy-done.1, f32[1,8192]{1,0:T(1,128)S(1)} %get-tuple-element.8.gain_ref), custom_call_target="tpu_custom_call" | custom-call | flops 150994944 | bytes 4718592 | tf_op jit(solution)/shard_map/finish/pallas_call | solution.py:183
  (10 shorter events, 0.2 us)
Async XLA Ops:
  0.0 21.9 %collective-permute-start.4 = (bf16[24,8192]{1,0:T(8,128)(2,1)}, bf16[24,8192]{1,0:T(8,128)(2,1)S(1)}, u32[]{:S(2)}, u32[]{:S(2)}) collective-permute-start(bf16[24,8192]{1,0:T(8,128)(2,1)} %param.6), channel_id=1, source_target_pairs={{0,1},{1,0},{2,3},{3,2},{4,5},{5,4},{6,7},{7,6},{8,9},{9,8},{10,11... | collective-permute-start | bytes 1179656 | tf_op jit(solution)/shard_map/ppermute | solution.py:203
  5.9 27.6 %collective-permute-start = (bf16[24,8192]{1,0:T(8,128)(2,1)}, bf16[24,8192]{1,0:T(8,128)(2,1)S(1)}, u32[]{:S(2)}, u32[]{:S(2)}) collective-permute-start(bf16[24,8192]{1,0:T(8,128)(2,1)} %param.6), channel_id=1, source_target_pairs={{0,4},{2,6},{4,8},{6,10},{8,12},{10,14},{12,0},{14,2},{1,5},{3,7},... | collective-permute-start | bytes 1179656 | tf_op jit(solution)/shard_map/ppermute | solution.py:19
  9.3 27.6 %collective-permute-start.1 = (bf16[24,8192]{1,0:T(8,128)(2,1)}, bf16[24,8192]{1,0:T(8,128)(2,1)S(1)}, u32[]{:S(2)}, u32[]{:S(2)}) collective-permute-start(bf16[24,8192]{1,0:T(8,128)(2,1)} %param.6), channel_id=1, source_target_pairs={{0,8},{2,10},{4,12},{6,14},{8,0},{10,2},{12,4},{14,6},{1,9},{3,11}... | collective-permute-start | bytes 1179656 | tf_op jit(solution)/shard_map/ppermute | solution.py:19
  14.0 38.2 %collective-permute-start.2 = (bf16[24,8192]{1,0:T(8,128)(2,1)}, bf16[24,8192]{1,0:T(8,128)(2,1)S(1)}, u32[]{:S(2)}, u32[]{:S(2)}) collective-permute-start(bf16[24,8192]{1,0:T(8,128)(2,1)} %param.6), channel_id=1, source_target_pairs={{0,12},{2,14},{4,0},{6,2},{8,4},{10,6},{12,8},{14,10},{1,13},{3,15... | collective-permute-start | bytes 1179656 | tf_op jit(solution)/shard_map/ppermute | solution.py:19
  21.9 17.3 %collective-permute-start.5 = (bf16[24,8192]{1,0:T(8,128)(2,1)S(1)}, bf16[24,8192]{1,0:T(8,128)(2,1)S(1)}, u32[]{:S(2)}, u32[]{:S(2)}) collective-permute-start(bf16[24,8192]{1,0:T(8,128)(2,1)S(1)} %collective-permute-done.4), channel_id=1, source_target_pairs={{0,4},{2,6},{4,8},{6,10},{8,12},{10,14},{12,0},{14,2},{1,5},{3,7},... | collective-permute-start | bytes 1179656 | tf_op jit(solution)/shard_map/ppermute | solution.py:19
  28.9 20.0 %collective-permute-start.6 = (bf16[24,8192]{1,0:T(8,128)(2,1)S(1)}, bf16[24,8192]{1,0:T(8,128)(2,1)S(1)}, u32[]{:S(2)}, u32[]{:S(2)}) collective-permute-start(bf16[24,8192]{1,0:T(8,128)(2,1)S(1)} %collective-permute-done.4), channel_id=1, source_target_pairs={{0,8},{2,10},{4,12},{6,14},{8,0},{10,2},{12,4},{14,6},{1,9},{3,11}... | collective-permute-start | bytes 1179656 | tf_op jit(solution)/shard_map/ppermute | solution.py:19
  33.5 16.7 %collective-permute-start.7 = (bf16[24,8192]{1,0:T(8,128)(2,1)S(1)}, bf16[24,8192]{1,0:T(8,128)(2,1)S(1)}, u32[]{:S(2)}, u32[]{:S(2)}) collective-permute-start(bf16[24,8192]{1,0:T(8,128)(2,1)S(1)} %collective-permute-done.4), channel_id=1, source_target_pairs={{0,12},{2,14},{4,0},{6,2},{8,4},{10,6},{12,8},{14,10},{1,13},{3,15... | collective-permute-start | bytes 1179656 | tf_op jit(solution)/shard_map/ppermute | solution.py:19
  37.0 17.7 %copy-start.4 = (bf16[512]{0:T(512)(128)(2,1)S(1)}, bf16[512]{0:T(512)(128)(2,1)}, u32[]{:S(2)}) copy-start(bf16[512]{0:T(512)(128)(2,1)} %param.8) | copy-start | bytes 3076
  50.2 15.4 %collective-permute-start.9 = (bf16[96,8192]{1,0:T(8,128)(2,1)S(1)}, bf16[96,8192]{1,0:T(8,128)(2,1)S(1)}, u32[]{:S(2)}, u32[]{:S(2)}) collective-permute-start(bf16[96,8192]{1,0:T(8,128)(2,1)S(1)} %constant_dynamic-update-slice_fusion.4.lhs_ref), channel_id=1, source_target_pairs={{0,2},{2,0},{4,6},{6,4},{8,10},{10,8},{12,14},{14,12},{1,3},{3,1},... | collective-permute-start | bytes 4718600 | tf_op jit(solution)/shard_map/ppermute | solution.py:24
  52.2 23.5 %collective-permute-start.3 = (bf16[96,8192]{1,0:T(8,128)(2,1)S(1)}, bf16[96,8192]{1,0:T(8,128)(2,1)S(1)}, u32[]{:S(2)}, u32[]{:S(2)}) collective-permute-start(bf16[96,8192]{1,0:T(8,128)(2,1)S(1)} %constant_dynamic-update-slice_fusion.lhs_ref), channel_id=1, source_target_pairs={{0,2},{2,0},{4,6},{6,4},{8,10},{10,8},{12,14},{14,12},{1,3},{3,1},... | collective-permute-start | bytes 4718600 | tf_op jit(solution)/shard_map/ppermute | solution.py:24
  54.7 3.4 %copy-start = (bf16[8192,512]{1,0:T(8,128)(2,1)S(1)}, bf16[8192,512]{1,0:T(8,128)(2,1)}, u32[]{:S(2)}) copy-start(bf16[8192,512]{1,0:T(8,128)(2,1)} %w_ref.7) | copy-start | bytes 25165828
  58.0 15.2 %slice-start = ((s8[8388608]{0:T(1024)(128)(4,1)}), s8[4194304]{0:T(1024)(128)(4,1)S(1)}, s32[]{:S(2)}) async-start(s8[8388608]{0:T(1024)(128)(4,1)} %bitcast.1), calls=%async_computation.2 | async-start | bytes 8388608
  60.6 12.6 %slice-start.1 = ((s8[8388608]{0:T(1024)(128)(4,1)}), s8[4194304]{0:T(1024)(128)(4,1)S(1)}, s32[]{:S(2)}) async-start(s8[8388608]{0:T(1024)(128)(4,1)} %bitcast.1), calls=%async_computation.3 | async-start | bytes 8388608
  60.6 17.6 %collective-permute-start.8 = (bf16[4,24,512]{2,1,0:T(8,128)(2,1)S(1)}, bf16[4,24,512]{2,1,0:T(8,128)(2,1)S(1)}, u32[]{:S(2)}, u32[]{:S(2)}) collective-permute-start(bf16[4,24,512]{2,1,0:T(8,128)(2,1)S(1)} %project.6), channel_id=1, source_target_pairs={{0,1},{1,0},{2,3},{3,2},{4,5},{5,4},{6,7},{7,6},{8,9},{9,8},{10,11... | collective-permute-start | bytes 294920 | tf_op jit(solution)/shard_map/ppermute | solution.py:214
  68.2 11.9 %collective-permute-start.10 = (bf16[4,24,512]{2,1,0:T(8,128)(2,1)S(1)}, bf16[4,24,512]{2,1,0:T(8,128)(2,1)S(1)}, u32[]{:S(2)}, u32[]{:S(2)}) collective-permute-start(bf16[4,24,512]{2,1,0:T(8,128)(2,1)S(1)} %project.7), channel_id=1, source_target_pairs={{0,1},{1,0},{2,3},{3,2},{4,5},{5,4},{6,7},{7,6},{8,9},{9,8},{10,11... | collective-permute-start | bytes 294920 | tf_op jit(solution)/shard_map/ppermute | solution.py:214
  78.2 6.6 %copy-start.3 = (bf16[8192]{0:T(1024)(128)(2,1)S(1)}, bf16[8192]{0:T(1024)(128)(2,1)}, u32[]{:S(2)}) copy-start(bf16[8192]{0:T(1024)(128)(2,1)} %param.11) | copy-start | bytes 49156
  78.2 6.6 %copy-start.2 = (s32[24,1]{0,1:T(1,128)S(1)}, s32[24,1]{0,1:T(1,128)}, u32[]{:S(2)}) copy-start(s32[24,1]{0,1:T(1,128)} %param.9) | copy-start | bytes 292
  80.9 12.8 %all-to-all-start = ((bf16[8,24,1024]{2,1,0:T(8,128)(2,1)}), bf16[8,24,1024]{2,1,0:T(8,128)(2,1)S(1)}, u32[]{:S(2)}, u32[]{:S(2)}) async-start(bf16[8,24,1024]{2,1,0:T(8,128)(2,1)} %join.1), calls=%async_computation | async-start | bytes 786432 | tf_op jit(solution)/shard_map/all_to_all | solution.py:225
  94.3 77.0 %copy-start.1 = (bf16[96,8192]{1,0:T(8,128)(2,1)S(1)}, bf16[96,8192]{1,0:T(8,128)(2,1)}, u32[]{:S(2)}) copy-start(bf16[96,8192]{1,0:T(8,128)(2,1)} %text_ref.1) | copy-start | bytes 4718596
